TPU v7x, 512 devices: a whole 4x8x8 slice. The times are simulated.
512 devices in a mesh: section: 8 (over z), expert: 16 (over y, core), dp: 4 (over x).
Axes of the slice: x: 4, y: 8, z: 8, core: 2. Of those that a mesh axis runs over, the one named last changes fastest.
Arguments:
- arrivals: bfloat16 [8, 4096, 2048], P('section', ('expert', 'dp')), may hold values from -6 to 6
- fresh: bfloat16 [1, 4096, 2048], P(None, ('expert', 'dp')), may hold values from -6 to 6
- routes: int32 [8, 2, 4096, 6], P('section', None, ('expert', 'dp')), may hold values from 0 to 63, as said below
- gates: bfloat16 [8, 2, 4096, 6], P('section', None, ('expert', 'dp')), may hold values from 0.099609375 to 1
- cotangent: bfloat16 [8, 2, 4096, 2048], P('section', None, ('expert', 'dp')), may hold values from -0.3125 to 0.3125
- norm_gain: float32 [8, 2048], P('section'), may hold values from 0.5 to 1.5
- w_gate: bfloat16 [8, 5632, 2048], P('section', 'expert', 'dp'), may hold values from -0.125 to 0.125
- w_up: bfloat16 [8, 5632, 2048], P('section', 'expert', 'dp'), may hold values from -0.125 to 0.125
- w_down: bfloat16 [8, 5632, 2048], P('section', 'expert', 'dp'), may hold values from -0.15625 to 0.15625
Outputs:
- layer_out: bfloat16 [8, 2, 4096, 2048], P('section', None, ('expert', 'dp'))
- grad_down: float32 [8, 5632, 2048], P('section', 'expert', 'dp')
Inputs may be any that keep to these rules, and one draw needn't show every extreme that they name: `routes`: each token's 6 entries are different expert numbers.
All inputs are finite; a program needn't handle non-finite values.
Results may differ from a plain program's by a relative error of at most 0.0085.
Values may be sent and summed in bfloat16 or wider, within the bound.
A program may use at most 64 MiB of HBM per device.

v0:
```python
import jax
import jax.numpy as jnp
from jax import lax
from jax.sharding import PartitionSpec as P

SPLIT = 4
CAP = 12


def in_one_piece(arrays, axis, dim, along):
    both = jnp.concatenate(arrays, axis=along)
    whole, at, gathered = (lax.all_gather(both, axis, axis=dim, tiled=True), 0, [])
    for a in arrays:
        gathered.append(lax.slice_in_dim(whole, at, at + a.shape[along], axis=along))
        at += a.shape[along]
    return tuple(gathered)


def shifted_2(shard, axis, by):
    count = lax.axis_size(axis)
    pairs = [(i, i + by) for i in range(count) if 0 <= i + by < count]
    return lax.ppermute(shard, axis, pairs)


def local(arrivals, fresh, routes, gates, cotangent, norm_gain, w_gate, w_up, w_down):
    n_expert = lax.axis_size("expert")
    flight = n_expert // SPLIT
    section_index = lax.axis_index("section")
    tok_rows = arrivals.shape[1]
    model_width = arrivals.shape[2]
    step_count = routes.shape[1]
    gains = norm_gain[0]
    gate_local, up_local, down_local = in_one_piece((w_gate[0], w_up[0], w_down[0]), "dp", 1, 0)
    hid_rows = gate_local.shape[0]
    slot_ids = jnp.arange(CAP, dtype=jnp.int32)
    expert_ids = jnp.arange(flight, dtype=jnp.int32)
    row_dims = (((0,), (0,)), ((), ()))

    def selection(step_index):
        routing = routes[0, step_index]
        weights = gates[0, step_index].astype(jnp.float32)
        matches = routing[:, :, None] == expert_ids[None, None, :]
        naming = jnp.any(matches, axis=1).astype(jnp.int32)
        shares = jnp.sum(jnp.where(matches, weights[:, :, None], 0.0), axis=1)
        places = jnp.cumsum(naming, axis=0) - naming
        chosen = (naming.T[:, None, :] == 1) & (places.T[:, None, :] == slot_ids[None, :, None])
        select = chosen.reshape(flight * CAP, tok_rows).astype(jnp.bfloat16)
        slot_gate = jnp.sum(jnp.where(chosen, shares.T[:, None, :], 0.0), axis=2).reshape(
            flight * CAP
        )
        counts = jnp.minimum(jnp.sum(naming, axis=0), CAP)
        return (select, slot_gate, counts)

    def fan_out(block_in):
        spread = jnp.broadcast_to(block_in[:, None], (flight, SPLIT) + block_in.shape[1:])
        return spread.reshape((n_expert,) + block_in.shape[1:])

    def pack_rows(select, values):
        rows = jnp.dot(select, values, preferred_element_type=jnp.float32).astype(jnp.bfloat16)
        return fan_out(rows.reshape(flight, CAP, model_width))

    picks = [selection(turn_num) for turn_num in range(step_count)]
    incoming = arrivals[0]
    grad_total = jnp.zeros((hid_rows, model_width), jnp.float32)
    outputs = []
    for turn_num in range(step_count):
        if turn_num > 0:
            shifted = shifted_2(outputs[-1], "section", 1)
            incoming = jnp.where(section_index == 0, fresh[turn_num - 1], shifted)
        floats = incoming.astype(jnp.float32)
        scale = lax.rsqrt(jnp.mean(floats * floats, axis=1, keepdims=True) + 0.5)
        normed = (floats * scale * gains[None, :]).astype(jnp.bfloat16)
        select, slot_gate, counts = picks[turn_num]
        send_tok = pack_rows(select, normed)
        send_cot = pack_rows(select, cotangent[0, turn_num])
        send_gate = fan_out(slot_gate.reshape(flight, CAP).astype(jnp.bfloat16))
        send_count = fan_out(counts)
        rows_tok, rows_cot, rows_gate, rows_count = (
            lax.all_to_all(send_tok, "expert", split_axis=0, concat_axis=0, tiled=True),
            lax.all_to_all(send_cot, "expert", split_axis=0, concat_axis=0, tiled=True),
            lax.all_to_all(send_gate, "expert", split_axis=0, concat_axis=0, tiled=True),
            lax.all_to_all(send_count, "expert", split_axis=0, concat_axis=0, tiled=True),
        )
        total_rows = n_expert * CAP
        flat_tok = rows_tok.reshape(total_rows, model_width)
        flat_cot = rows_cot.reshape(total_rows, model_width)
        flat_gate = rows_gate.reshape(total_rows)
        dims = (((1,), (1,)), ((), ()))
        gate_act = lax.dot_general(flat_tok, gate_local, dims, preferred_element_type=jnp.float32)
        up_act = lax.dot_general(flat_tok, up_local, dims, preferred_element_type=jnp.float32)
        hidden = (jax.nn.silu(gate_act) * up_act).astype(jnp.bfloat16)
        partial_value = jnp.dot(hidden, down_local, preferred_element_type=jnp.float32).astype(
            jnp.bfloat16
        )
        weighted = (hidden.astype(jnp.float32) * flat_gate.astype(jnp.float32)[:, None]).astype(
            jnp.bfloat16
        )
        expert_partial_value = partial_value
        grad_add = lax.dot_general(weighted, flat_cot, row_dims, preferred_element_type=jnp.float32)
        partial_value, grad_add = (
            expert_partial_value.reshape(n_expert, CAP, model_width),
            grad_add,
        )
        returned = lax.all_to_all(partial_value, "expert", split_axis=0, concat_axis=0, tiled=True)
        expert_out = jnp.sum(
            returned.reshape(flight, SPLIT, CAP, model_width).astype(jnp.float32), axis=1
        ).reshape(flight * CAP, model_width)
        mixing = select.astype(jnp.float32).T * slot_gate[None, :]
        mixture = jnp.dot(mixing, expert_out)
        result = (floats + mixture).astype(jnp.bfloat16)
        outputs.append(result)
        grad_total = grad_total + grad_add
    grad_part = lax.psum_scatter(grad_total, "dp", scatter_dimension=1, tiled=True)
    return (jnp.stack(outputs)[None], grad_part[None])


def solution(mesh):
    placed = (
        P("section", ("expert", "dp"), None),
        P(None, ("expert", "dp"), None),
        P("section", None, ("expert", "dp"), None),
        P("section", None, ("expert", "dp"), None),
        P("section", None, ("expert", "dp"), None),
        P("section", None),
        P("section", "expert", "dp"),
        P("section", "expert", "dp"),
        P("section", "expert", "dp"),
    )
    return jax.shard_map(
        local,
        mesh=mesh,
        in_specs=placed,
        out_specs=(P("section", None, ("expert", "dp"), None), P("section", "expert", "dp")),
        check_vma=False,
    )
```

profile of v0, /device:TPU:1, one launch (start us, length us, event | category | flops | bytes accessed | tf_op | source)
XLA Modules:
  0.0 257.4 jit_solution(1470381803532542575)
XLA Ops:
  7.3 2.3 pad_maximum_fusion
  10.8 10.1 %all-to-all-start.4 = ((bf16[16,1,12]{2,1,0:T(2,128)(2,1)}), bf16[16,1,12]{2,1,0:T(2,128)(2,1)S(1)}, u32[]{:S(2)}, u32[]{:S(2)}) async-start(bf16[16,1,12]{2,1,0:T(2,128)(2,1)} %copy.67), calls=%async_computation.4 | async-start | bytes 16384 | tf_op jit(solution)/shard_map/all_to_all | solution.py:81
  22.3 5.6 %all-to-all-done.4 = bf16[16,1,12]{2,1,0:T(2,128)(2,1)S(1)} async-done(((bf16[16,1,12]{2,1,0:T(2,128)(2,1)}), bf16[16,1,12]{2,1,0:T(2,128)(2,1)S(1)}, u32[]{:S(2)}, u32[]{:S(2)}) %all-to-all-start.4) | async-done | bytes 416 | tf_op jit(solution)/shard_map/all_to_all | solution.py:81
  27.9 3.9 %all-to-all-start.6 = ((bf16[16,1,12]{2,1,0:T(2,128)(2,1)}), bf16[16,1,12]{2,1,0:T(2,128)(2,1)S(1)}, u32[]{:S(2)}, u32[]{:S(2)}) async-start(bf16[16,1,12]{2,1,0:T(2,128)(2,1)} %copy.68), calls=%async_computation.6 | async-start | bytes 16384 | tf_op jit(solution)/shard_map/all_to_all | solution.py:81
  32.2 6.7 %all-to-all-done.6 = bf16[16,1,12]{2,1,0:T(2,128)(2,1)S(1)} async-done(((bf16[16,1,12]{2,1,0:T(2,128)(2,1)}), bf16[16,1,12]{2,1,0:T(2,128)(2,1)S(1)}, u32[]{:S(2)}, u32[]{:S(2)}) %all-to-all-start.6) | async-done | bytes 416 | tf_op jit(solution)/shard_map/all_to_all | solution.py:81
  40.0 4.1 %all-to-all-start = ((bf16[16,12,2048]{2,1,0:T(8,128)(2,1)}), bf16[16,12,2048]{2,1,0:T(8,128)(2,1)S(1)}, u32[]{:S(2)}, u32[]{:S(2)}) async-start(bf16[16,12,2048]{2,1,0:T(8,128)(2,1)} %bitcast.8), calls=%async_computation | async-start | bytes 2097152 | tf_op jit(solution)/shard_map/all_to_all | solution.py:79
  44.4 27.8 %all-to-all-done = bf16[16,12,2048]{2,1,0:T(8,128)(2,1)S(1)} async-done(((bf16[16,12,2048]{2,1,0:T(8,128)(2,1)}), bf16[16,12,2048]{2,1,0:T(8,128)(2,1)S(1)}, u32[]{:S(2)}, u32[]{:S(2)}) %all-to-all-start) | async-done | bytes 786464 | tf_op jit(solution)/shard_map/all_to_all | solution.py:79
  73.3 3.5 %all-to-all-start.5 = ((bf16[16,12,2048]{2,1,0:T(8,128)(2,1)}), bf16[16,12,2048]{2,1,0:T(8,128)(2,1)S(1)}, u32[]{:S(2)}, u32[]{:S(2)}) async-start(bf16[16,12,2048]{2,1,0:T(8,128)(2,1)} %bitcast.26), calls=%async_computation.5 | async-start | bytes 2097152 | tf_op jit(solution)/shard_map/all_to_all | solution.py:80
  77.1 2.0 fusion.11
  79.1 2.0 fusion.22
  81.2 1.9 convolution_convert_fusion.1
  83.1 1.1 reshape.240
  84.2 20.5 %all-to-all-done.5 = bf16[16,12,2048]{2,1,0:T(8,128)(2,1)S(1)} async-done(((bf16[16,12,2048]{2,1,0:T(8,128)(2,1)}), bf16[16,12,2048]{2,1,0:T(8,128)(2,1)S(1)}, u32[]{:S(2)}, u32[]{:S(2)}) %all-to-all-start.5) | async-done | bytes 786464 | tf_op jit(solution)/shard_map/all_to_all | solution.py:80
  104.7 3.6 %all-to-all-start.1 = ((bf16[16,12,2048]{2,1,0:T(8,128)(2,1)}), bf16[16,12,2048]{2,1,0:T(8,128)(2,1)S(1)}, u32[]{:S(2)}, u32[]{:S(2)}) async-start(bf16[16,12,2048]{2,1,0:T(8,128)(2,1)} %reshape.240), calls=%async_computation.1 | async-start | bytes 2097152 | tf_op jit(solution)/shard_map/all_to_all | solution.py:104
  108.6 27.5 %all-to-all-done.1 = bf16[16,12,2048]{2,1,0:T(8,128)(2,1)S(1)} async-done(((bf16[16,12,2048]{2,1,0:T(8,128)(2,1)}), bf16[16,12,2048]{2,1,0:T(8,128)(2,1)S(1)}, u32[]{:S(2)}, u32[]{:S(2)}) %all-to-all-start.1) | async-done | bytes 786464 | tf_op jit(solution)/shard_map/all_to_all | solution.py:104
  137.2 3.5 %all-to-all-start.7 = ((bf16[16,12,2048]{2,1,0:T(8,128)(2,1)}), bf16[16,12,2048]{2,1,0:T(8,128)(2,1)S(1)}, u32[]{:S(2)}, u32[]{:S(2)}) async-start(bf16[16,12,2048]{2,1,0:T(8,128)(2,1)} %bitcast.29), calls=%async_computation.7 | async-start | bytes 2097152 | tf_op jit(solution)/shard_map/all_to_all | solution.py:80
  143.5 1.3 fusion
  144.8 2.5 collective-permute-start
  149.4 3.6 %collective-permute-done = bf16[64,2048]{1,0:T(8,128)(2,1)S(1)} collective-permute-done((bf16[64,2048]{1,0:T(8,128)(2,1)S(1)}, bf16[64,2048]{1,0:T(8,128)(2,1)S(1)}, u32[]{:S(2)}, u32[]{:S(2)}) %collective-permute-start) | collective-permute-done | bytes 262176 | tf_op jit(solution)/shard_map/ppermute | solution.py:22
  153.0 1.1 fusion.29
  155.2 13.5 %all-to-all-done.7 = bf16[16,12,2048]{2,1,0:T(8,128)(2,1)S(1)} async-done(((bf16[16,12,2048]{2,1,0:T(8,128)(2,1)}), bf16[16,12,2048]{2,1,0:T(8,128)(2,1)S(1)}, u32[]{:S(2)}, u32[]{:S(2)}) %all-to-all-start.7) | async-done | bytes 786464 | tf_op jit(solution)/shard_map/all_to_all | solution.py:80
  169.8 4.2 %all-to-all-start.2 = ((bf16[16,12,2048]{2,1,0:T(8,128)(2,1)}), bf16[16,12,2048]{2,1,0:T(8,128)(2,1)}, u32[]{:S(2)}, u32[]{:S(2)}) async-start(bf16[16,12,2048]{2,1,0:T(8,128)(2,1)} %bitcast.20), calls=%async_computation.2 | async-start | bytes 2097152 | tf_op jit(solution)/shard_map/all_to_all | solution.py:79
  177.6 1.8 fusion.43
  179.4 21.9 %all-to-all-done.2 = bf16[16,12,2048]{2,1,0:T(8,128)(2,1)} async-done(((bf16[16,12,2048]{2,1,0:T(8,128)(2,1)}), bf16[16,12,2048]{2,1,0:T(8,128)(2,1)}, u32[]{:S(2)}, u32[]{:S(2)}) %all-to-all-start.2) | async-done | bytes 786464 | tf_op jit(solution)/shard_map/all_to_all | solution.py:79
  201.2 2.1 reshape.243
  203.4 2.3 fusion.9
  205.8 2.1 fusion.19
  207.9 2.3 convolution_add_fusion
  210.2 1.9 convolution_convert_fusion
  213.3 3.7 %all-to-all-start.3 = ((bf16[16,12,2048]{2,1,0:T(8,128)(2,1)}), bf16[16,12,2048]{2,1,0:T(8,128)(2,1)S(1)}, u32[]{:S(2)}, u32[]{:S(2)}) async-start(bf16[16,12,2048]{2,1,0:T(8,128)(2,1)} %reshape.244), calls=%async_computation.3 | async-start | bytes 2097152 | tf_op jit(solution)/shard_map/all_to_all | solution.py:104
  217.1 27.8 %all-to-all-done.3 = bf16[16,12,2048]{2,1,0:T(8,128)(2,1)S(1)} async-done(((bf16[16,12,2048]{2,1,0:T(8,128)(2,1)}), bf16[16,12,2048]{2,1,0:T(8,128)(2,1)S(1)}, u32[]{:S(2)}, u32[]{:S(2)}) %all-to-all-start.3) | async-done | bytes 786464 | tf_op jit(solution)/shard_map/all_to_all | solution.py:104
  246.3 4.2 %reduce-scatter.2.cloned.1.call-done = f32[352,512]{1,0:T(8,128)} async-done(((f32[352,2048]{1,0:T(8,128)}), f32[352,512]{1,0:T(8,128)}) %reduce-scatter.2.cloned.1.call-update) | async-done | bytes 720912 | tf_op jit(solution)/shard_map/reduce_scatter | solution.py:113
  (117 shorter events, 20.1 us)
Async XLA Ops:
  7.2 2.4 copy-start.16
  7.2 2.8 %copy-start.14 = (bf16[1,2,64,6]{2,1,3,0:T(2,128)(2,1)S(1)}, bf16[1,2,64,6]{2,1,3,0:T(2,128)(2,1)}, u32[]{:S(2)}) copy-start(bf16[1,2,64,6]{2,1,3,0:T(2,128)(2,1)} %param.12) | copy-start | bytes 4612
  7.2 14.2 %copy-start.1 = (bf16[1,64,2048]{2,1,0:T(8,128)(2,1)S(1)}, bf16[1,64,2048]{2,1,0:T(8,128)(2,1)}, u32[]{:S(2)}) copy-start(bf16[1,64,2048]{2,1,0:T(8,128)(2,1)} %param.9) | copy-start | bytes 786436
  7.2 24.6 %copy-start.18 = (f32[1,2048]{1,0:T(1,128)S(1)}, f32[1,2048]{1,0:T(1,128)}, u32[]{:S(2)}) copy-start(f32[1,2048]{1,0:T(1,128)} %param.14) | copy-start | bytes 24580
  7.2 69.9 %all-gather.2.cloned.1.call-start = ((), (), s32[]{:S(2)}) async-start(), calls=%async_computation.9 | async-start | bytes 5406720 | tf_op jit(solution)/shard_map/all_gather | solution.py:12
  10.8 17.1 %all-to-all-start.4 = ((bf16[16,1,12]{2,1,0:T(2,128)(2,1)}), bf16[16,1,12]{2,1,0:T(2,128)(2,1)S(1)}, u32[]{:S(2)}, u32[]{:S(2)}) async-start(bf16[16,1,12]{2,1,0:T(2,128)(2,1)} %copy.67), calls=%async_computation.4 | async-start | bytes 16384 | tf_op jit(solution)/shard_map/all_to_all | solution.py:81
  21.1 87.1 %copy-start.15 = (pred[4,64]{1,0:T(4,128)(4,1)}, pred[4,64]{1,0:T(4,128)(4,1)S(1)}, u32[]{:S(2)}) copy-start(pred[4,64]{1,0:T(4,128)(4,1)S(1)} %copy.64) | copy-start | bytes 772
  21.3 87.0 %copy-start.5 = (s32[4,64]{1,0:T(4,128)}, s32[4,64]{1,0:T(4,128)S(1)}, u32[]{:S(2)}) copy-start(s32[4,64]{1,0:T(4,128)S(1)} %copy.65) | copy-start | bytes 3076
  21.6 18.4 %copy-start.12 = (f32[4,12]{1,0:T(4,128)}, f32[4,12]{1,0:T(4,128)S(1)}, u32[]{:S(2)}) copy-start(f32[4,12]{1,0:T(4,128)S(1)} %select_reduce_fusion) | copy-start | bytes 580
  27.9 12.1 %copy-start.6 = (bf16[16,1,12]{2,1,0:T(2,128)(2,1)}, bf16[16,1,12]{2,1,0:T(2,128)(2,1)S(1)}, u32[]{:S(2)}) copy-start(bf16[16,1,12]{2,1,0:T(2,128)(2,1)S(1)} %all-to-all-done.4) | copy-start | bytes 1156
  27.9 11.0 %all-to-all-start.6 = ((bf16[16,1,12]{2,1,0:T(2,128)(2,1)}), bf16[16,1,12]{2,1,0:T(2,128)(2,1)S(1)}, u32[]{:S(2)}, u32[]{:S(2)}) async-start(bf16[16,1,12]{2,1,0:T(2,128)(2,1)} %copy.68), calls=%async_computation.6 | async-start | bytes 16384 | tf_op jit(solution)/shard_map/all_to_all | solution.py:81
  31.8 12.3 %copy-start.3 = (bf16[1,2,64,2048]{3,2,1,0:T(8,128)(2,1)S(1)}, bf16[1,2,64,2048]{3,2,1,0:T(8,128)(2,1)}, u32[]{:S(2)}) copy-start(bf16[1,2,64,2048]{3,2,1,0:T(8,128)(2,1)} %param.13) | copy-start | bytes 1572868
  38.9 5.5 %copy-start.8 = (bf16[16,1,12]{2,1,0:T(2,128)(2,1)}, bf16[16,1,12]{2,1,0:T(2,128)(2,1)S(1)}, u32[]{:S(2)}) copy-start(bf16[16,1,12]{2,1,0:T(2,128)(2,1)S(1)} %all-to-all-done.6) | copy-start | bytes 1156
  40.0 32.1 %all-to-all-start = ((bf16[16,12,2048]{2,1,0:T(8,128)(2,1)}), bf16[16,12,2048]{2,1,0:T(8,128)(2,1)S(1)}, u32[]{:S(2)}, u32[]{:S(2)}) async-start(bf16[16,12,2048]{2,1,0:T(8,128)(2,1)} %bitcast.8), calls=%async_computation | async-start | bytes 2097152 | tf_op jit(solution)/shard_map/all_to_all | solution.py:79
  73.3 31.4 %all-to-all-start.5 = ((bf16[16,12,2048]{2,1,0:T(8,128)(2,1)}), bf16[16,12,2048]{2,1,0:T(8,128)(2,1)S(1)}, u32[]{:S(2)}, u32[]{:S(2)}) async-start(bf16[16,12,2048]{2,1,0:T(8,128)(2,1)} %bitcast.26), calls=%async_computation.5 | async-start | bytes 2097152 | tf_op jit(solution)/shard_map/all_to_all | solution.py:80
  84.2 24.1 %copy-start.4 = (bf16[1,2,64,2048]{3,2,1,0:T(8,128)(2,1)S(1)}, bf16[1,2,64,2048]{3,2,1,0:T(8,128)(2,1)}, u32[]{:S(2)}) copy-start(bf16[1,2,64,2048]{3,2,1,0:T(8,128)(2,1)} %param.13) | copy-start | bytes 1572868
  104.7 31.4 %all-to-all-start.1 = ((bf16[16,12,2048]{2,1,0:T(8,128)(2,1)}), bf16[16,12,2048]{2,1,0:T(8,128)(2,1)S(1)}, u32[]{:S(2)}, u32[]{:S(2)}) async-start(bf16[16,12,2048]{2,1,0:T(8,128)(2,1)} %reshape.240), calls=%async_computation.1 | async-start | bytes 2097152 | tf_op jit(solution)/shard_map/all_to_all | solution.py:104
  137.2 31.4 %all-to-all-start.7 = ((bf16[16,12,2048]{2,1,0:T(8,128)(2,1)}), bf16[16,12,2048]{2,1,0:T(8,128)(2,1)S(1)}, u32[]{:S(2)}, u32[]{:S(2)}) async-start(bf16[16,12,2048]{2,1,0:T(8,128)(2,1)} %bitcast.29), calls=%async_computation.7 | async-start | bytes 2097152 | tf_op jit(solution)/shard_map/all_to_all | solution.py:80
  144.8 8.1 %collective-permute-start = (bf16[64,2048]{1,0:T(8,128)(2,1)S(1)}, bf16[64,2048]{1,0:T(8,128)(2,1)S(1)}, u32[]{:S(2)}, u32[]{:S(2)}) collective-permute-start(bf16[64,2048]{1,0:T(8,128)(2,1)S(1)} %fusion), channel_id=1, source_target_pairs={{0,64},{64,128},{128,192},{192,256},{256,320},{320,384},{384,448},... | collective-permute-start | bytes 786440 | tf_op jit(solution)/shard_map/ppermute | solution.py:22
  149.4 20.4 %copy-start.10 = (pred[48,64]{1,0:T(8,128)(4,1)}, pred[48,64]{1,0:T(8,128)(4,1)S(1)}, u32[]{:S(2)}) copy-start(pred[48,64]{1,0:T(8,128)(4,1)S(1)} %compare_and_fusion) | copy-start | bytes 9220
  154.1 20.0 %copy-start.7 = (bf16[16,1,12]{2,1,0:T(2,128)(2,1)S(1)}, bf16[16,1,12]{2,1,0:T(2,128)(2,1)}, u32[]{:S(2)}) copy-start(bf16[16,1,12]{2,1,0:T(2,128)(2,1)} %copy-done.6) | copy-start | bytes 1156
  154.1 20.7 %copy-start.9 = (bf16[16,1,12]{2,1,0:T(2,128)(2,1)S(1)}, bf16[16,1,12]{2,1,0:T(2,128)(2,1)}, u32[]{:S(2)}) copy-start(bf16[16,1,12]{2,1,0:T(2,128)(2,1)} %copy-done.8) | copy-start | bytes 1156
  169.8 31.5 %all-to-all-start.2 = ((bf16[16,12,2048]{2,1,0:T(8,128)(2,1)}), bf16[16,12,2048]{2,1,0:T(8,128)(2,1)}, u32[]{:S(2)}, u32[]{:S(2)}) async-start(bf16[16,12,2048]{2,1,0:T(8,128)(2,1)} %bitcast.20), calls=%async_computation.2 | async-start | bytes 2097152 | tf_op jit(solution)/shard_map/all_to_all | solution.py:79
  174.0 76.5 %reduce-scatter.2.cloned.1.call-start = ((), (), s32[]{:S(2)}) async-start(), calls=%async_computation.10 | async-start | bytes 3604480 | tf_op jit(solution)/shard_map/reduce_scatter | solution.py:113
  203.4 2.4 copy-start.2
  205.7 2.1 copy-start
  205.8 2.1 copy-start.17
  212.1 4.8 %copy-start.13 = (f32[4,12]{1,0:T(4,128)S(1)}, f32[4,12]{1,0:T(4,128)}, u32[]{:S(2)}) copy-start(f32[4,12]{1,0:T(4,128)} %copy-done.12) | copy-start | bytes 580
  213.3 31.9 %copy-start.11 = (pred[48,64]{1,0:T(8,128)(4,1)S(1)}, pred[48,64]{1,0:T(8,128)(4,1)}, u32[]{:S(2)}) copy-start(pred[48,64]{1,0:T(8,128)(4,1)} %copy-done.10) | copy-start | bytes 9220
  213.3 31.6 %all-to-all-start.3 = ((bf16[16,12,2048]{2,1,0:T(8,128)(2,1)}), bf16[16,12,2048]{2,1,0:T(8,128)(2,1)S(1)}, u32[]{:S(2)}, u32[]{:S(2)}) async-start(bf16[16,12,2048]{2,1,0:T(8,128)(2,1)} %reshape.244), calls=%async_computation.3 | async-start | bytes 2097152 | tf_op jit(solution)/shard_map/all_to_all | solution.py:104
Sparse Core Ops, SparseCore 0:
  10.1 59.9 all-gather.1
  210.3 40.2 reduce-scatter.1
where the time goes:
time: 259 us; the launch traced here: 257 us
  waiting for transfers between devices  159 us (61%)
  starting transfers between devices  39.2 us (15%)
  matrix products  19.7 us (8%)
  local copies, waits for them, and re-layouts  18.6 us (7%)
  between operations  14.6 us (6%)
  other arithmetic  6.09 us (2%)
    all_to_all x2, waiting for transfers between devices, local(): lax.all_to_all(partial_value, 'expert', split_axis=0, concat_axis=0, tile...  55.4 us
    all_to_all x2, waiting for transfers between devices, local(): lax.all_to_all(send_tok, 'expert', split_axis=0, concat_axis=0, tiled=True)  49.6 us
    all_to_all x2, waiting for transfers between devices, local(): lax.all_to_all(send_cot, 'expert', split_axis=0, concat_axis=0, tiled=True)  34 us
    all_to_all x2, starting transfers between devices, local(): lax.all_to_all(send_gate, 'expert', split_axis=0, concat_axis=0, tiled=True)  14 us
    all_to_all x2, waiting for transfers between devices, local(): lax.all_to_all(send_gate, 'expert', split_axis=0, concat_axis=0, tiled=True)  12.3 us
    all_to_all x2, starting transfers between devices, local(): lax.all_to_all(send_tok, 'expert', split_axis=0, concat_axis=0, tiled=True)  8.34 us
    all_to_all x2, starting transfers between devices, local(): lax.all_to_all(partial_value, 'expert', split_axis=0, concat_axis=0, tile...  7.23 us
    all_to_all x2, starting transfers between devices, local(): lax.all_to_all(send_cot, 'expert', split_axis=0, concat_axis=0, tiled=True)  7.1 us
  transfers between devices with their start and end apart: 11, of which 10 were waited for; matrix products, arithmetic and copies ran while one was open for 12% of the time, Pallas kernels for 0%

commit v1 on v0

v1 whole, which is shorter than its diff:
```python
import functools

import jax
import jax.numpy as jnp
from jax import lax
from jax.experimental import pallas as pl
from jax.experimental.pallas import tpu as pltpu
from jax.sharding import PartitionSpec as P

SPLIT = 4
CAP = 12
SLOTS = 16
MESH = pl.DeviceIdType.MESH
NT = (((1,), (1,)), ((), ()))
TN = (((0,), (0,)), ((), ()))
F32 = jnp.float32
BF16 = jnp.bfloat16


def kernel_body(
    nsec, nexp, ndp,
    arr, fresh, routes, gates, cot, gain, wg, wu, wd,
    out, grad_out,
    xin, cin, wbuf, tsend, trecv, csend, crecv, cotx, hid, dsend, drecv, rsend, rrecv,
    mix, obuf, gacc,
    lsem, wss, wrs, fss, frs, tss, trs, tds, tdr, css, crs, cxs, cxr, cds, cdr,
    hss, hrs, dss, drs, rss, rrs, zss, zrs,
):
    s = lax.axis_index("section")
    i = lax.axis_index("expert")
    d = lax.axis_index("dp")
    ny = nexp // 2
    y = lax.div(i, 2)
    c = lax.rem(i, 2)
    tok, width = arr.shape
    hidn, cols = wg.shape
    half = hidn // 2
    flight = nexp // SPLIT
    rows = flight * SLOTS

    def at_x(k):
        return (s, i, lax.rem(d + k, ndp))

    def at_y(k):
        return (s, lax.rem(y + k, ny) * 2 + c, d)

    def ysrc(k):
        return lax.rem(y + ny - k, ny)

    partner = (s, y * 2 + 1 - c, d)

    def colsl(x):
        return pl.ds(pl.multiple_of(x * cols, cols), cols)

    def rc(src, dst, ss, rs, dev):
        return pltpu.make_async_remote_copy(
            src_ref=src, dst_ref=dst, send_sem=ss, recv_sem=rs, device_id=dev, device_id_type=MESH
        )

    sends = []

    def go(cp):
        cp.start()
        sends.append(cp)
        return cp

    l_arr = pltpu.make_async_copy(arr, xin.at[0], lsem.at[0])
    l_cot = pltpu.make_async_copy(cot, cin, lsem.at[1])
    l_w = [
        pltpu.make_async_copy(w, wbuf.at[m, :, colsl(d)], lsem.at[2 + m])
        for m, w in enumerate((wg, wu, wd))
    ]
    l_fresh = pltpu.make_async_copy(fresh, xin.at[1], lsem.at[5])
    l_arr.start()
    for l in l_w:
        l.start()
    l_cot.start()

    @pl.when(s == 0)
    def _():
        l_fresh.start()

    bar = pltpu.get_barrier_semaphore()
    peers = [at_x(k) for k in range(1, ndp)] + [at_y(k) for k in range(1, ny)] + [partner]
    for p in peers:
        pl.semaphore_signal(bar, inc=1, device_id=p, device_id_type=MESH)

    @pl.when(s > 0)
    def _():
        pl.semaphore_signal(bar, inc=1, device_id=(s - 1, i, d), device_id_type=MESH)

    @pl.when(s < nsec - 1)
    def _():
        pl.semaphore_signal(bar, inc=1, device_id=(s + 1, i, d), device_id_type=MESH)

    slot = lax.rem(lax.broadcasted_iota(jnp.int32, (rows, tok), 0), SLOTS)
    ia = lax.broadcasted_iota(jnp.int32, (tok, tok), 0)
    ib = lax.broadcasted_iota(jnp.int32, (tok, tok), 1)
    before = (ia < ib).astype(F32).astype(BF16)
    eye = (ia == ib).astype(F32).astype(BF16)
    sels, selgs = [], []
    for k in range(2):
        r = routes[k]
        g = gates[k]
        names, shares = [], []
        for e in range(flight):
            m = r == e
            nm = jnp.max(jnp.where(m, 1.0, 0.0), axis=0, keepdims=True)
            sh = jnp.sum(jnp.where(m, g, 0.0), axis=0, keepdims=True)
            names.append(jnp.broadcast_to(nm, (SLOTS, tok)))
            shares.append(jnp.broadcast_to(sh, (SLOTS, tok)))
        naming = jnp.concatenate(names, axis=0)
        share = jnp.concatenate(shares, axis=0)
        places = jnp.dot(naming.astype(BF16), before, preferred_element_type=F32)
        chosen = (naming > 0.5) & (jnp.abs(places - slot.astype(F32)) < 0.5) & (slot < CAP)
        sel = jnp.where(chosen, 1.0, 0.0).astype(BF16)
        selg = jnp.where(chosen, share, 0.0).astype(BF16)
        sels.append(sel)
        selgs.append(selg)
        g3 = selg.reshape(flight, 1, SLOTS, tok)
        g3 = jnp.concatenate([g3, g3], axis=1).reshape(2 * rows, tok)
        mix[k] = lax.dot_general(eye, g3, NT, preferred_element_type=F32).astype(BF16)

    pl.semaphore_wait(
        bar,
        len(peers) + jnp.where(s > 0, 1, 0) + jnp.where(s < nsec - 1, 1, 0),
    )

    def send_w(m, w):
        for j, k in enumerate((1, ndp - 1)):
            go(rc(w, wbuf.at[m, :, colsl(d)], wss.at[m, j], wrs.at[m, j], at_x(k)))

    def forward_w(m, w):
        for j, k in enumerate((1, ndp - 1)):
            owner = lax.rem(d + ndp - k, ndp)
            rc(w, wbuf.at[m, :, colsl(owner)], wss.at[m, j], wrs.at[m, j], at_x(k)).wait_recv()
            part = wbuf.at[m, pl.ds(j * half, half), colsl(owner)]
            go(rc(part, part, fss.at[m, j], frs.at[m, j], at_x(k)))

    def wait_far(m):
        owner = lax.rem(d + 2, ndp)
        for j, k in enumerate((1, ndp - 1)):
            part = wbuf.at[m, pl.ds(j * half, half), colsl(owner)]
            rc(part, part, fss.at[m, j], frs.at[m, j], at_x(k)).wait_recv()

    send_w(0, wg)
    send_w(1, wu)

    gains = gain[...]

    def dispatch(k):
        x = xin[k].astype(F32)
        scale = lax.rsqrt(jnp.mean(x * x, axis=1, keepdims=True) + 0.5)
        normed = (x * scale * gains).astype(BF16)
        picked = jnp.dot(sels[k], normed, preferred_element_type=F32).astype(BF16)
        tsend[k] = picked.reshape(flight, SLOTS, width)
        own = tsend.at[k, lax.div(y, 2)]
        for n in range(1, ny):
            dest = lax.rem(y + n, ny)
            go(rc(tsend.at[k, lax.div(dest, 2)], trecv.at[k, 0, y], tss.at[k, n], trs.at[k, n], at_y(n)))
        go(rc(own, trecv.at[k, 1, y], tds.at[k, 0], tdr.at[k, 0], partner))
        trecv[k, 0, y] = tsend[k, lax.div(y, 2)]

    def spread(k):
        for n in range(1, ny):
            blk = trecv.at[k, 0, ysrc(n)]
            rc(blk, blk, tss.at[k, n], trs.at[k, n], at_y(n)).wait_recv()
            go(rc(blk, trecv.at[k, 1, ysrc(n)], tds.at[k, n], tdr.at[k, n], partner))
    def wait_spread(k):
        for n in range(ny):
            blk = trecv.at[k, 1, ysrc(n)]
            rc(blk, blk, tds.at[k, n], tdr.at[k, n], partner).wait_recv()

    l_arr.wait()
    dispatch(0)

    l_cot.wait()
    for k in range(2):
        picked = jnp.dot(selgs[k], cin[k], preferred_element_type=F32).astype(BF16)
        csend[:, pl.ds(k * SLOTS, SLOTS), :] = picked.reshape(flight, SLOTS, width)
    for n in range(1, ny):
        dest = lax.rem(y + n, ny)
        go(rc(csend.at[lax.div(dest, 2)], crecv.at[y], css.at[n], crs.at[n], at_y(n)))
    crecv[y] = csend[lax.div(y, 2)]

    forward_w(0, wg)
    spread(0)
    forward_w(1, wu)
    send_w(2, wd)
    wait_spread(0)

    def gate_up(k):
        x = trecv[k].reshape(nexp * SLOTS, width)
        ga = lax.dot_general(wbuf[0], x, NT, preferred_element_type=F32)
        ua = lax.dot_general(wbuf[1], x, NT, preferred_element_type=F32)
        h = (ga / (1.0 + jnp.exp(-ga)) * ua).astype(BF16)
        hid[k, d] = h
        for n in range(1, ndp):
            go(rc(hid.at[k, d], hid.at[k, d], hss.at[k, n], hrs.at[k, n], at_x(n)))
        return h

    def down(k, h):
        hrows = nexp * SLOTS // 2

        def finish(r):
            rc(dsend.at[k, r], drecv.at[k, r], dss.at[k, r], drs.at[k, r], partner).wait_recv()
            total = (rsend[k, r].reshape(hrows, cols).astype(F32) + drecv[k, r].astype(F32)).astype(BF16)
            rsend[k, r] = total.reshape(ny, SLOTS, cols)
            for n in range(1, ny):
                go(rc(rsend.at[k, r, lax.rem(y + n, ny)], rrecv.at[k, r, y], rss.at[k, r, n], rrs.at[k, r, n], at_y(n)))
            rrecv[k, r, y] = rsend[k, r, y]

        for r in range(ndp):
            if k == 0 and r == 1:
                forward_w(2, wd)
            if k == 0 and r == 3:
                wait_far(2)
            off = (0, 1, 3, 2)[r]
            x = lax.rem(d + off, ndp)
            part = lax.dot_general(h, wbuf[2, :, colsl(x)], TN, preferred_element_type=F32).astype(BF16)
            dsend[k, r] = part[hrows:]
            go(rc(dsend.at[k, r], drecv.at[k, r], dss.at[k, r], drs.at[k, r], partner))
            rsend[k, r] = part[:hrows].reshape(ny, SLOTS, cols)
            if r > 0:
                finish(r - 1)
        finish(ndp - 1)

    def combine(k):
        for r in range(ndp):
            off = (0, 1, 3, 2)[r]
            cs = colsl(lax.rem(d + off, ndp))
            for n in range(1, ny):
                blk = rrecv.at[k, r, ysrc(n)]
                rc(blk, blk, rss.at[k, r, n], rrs.at[k, r, n], at_y(n)).wait_recv()
            got = rrecv[k, r].reshape(ny * SLOTS, cols)
            res = xin[k, :, cs].astype(F32) + jnp.dot(mix[k], got, preferred_element_type=F32)
            obuf[k, :, cs] = res.astype(BF16)
            if k == 0:
                @pl.when(s < nsec - 1)
                def _():
                    rc(obuf.at[0, :, cs], xin.at[1, :, cs], zss.at[r], zrs.at[r], (s + 1, i, d)).start()

    l_w[0].wait()
    l_w[1].wait()
    wait_far(0)
    wait_far(1)
    h0 = gate_up(0)
    l_w[2].wait()
    down(0, h0)

    for n in range(1, ny):
        blk = crecv.at[ysrc(n)]
        rc(blk, blk, css.at[n], crs.at[n], at_y(n)).wait_recv()
    for n in range(1, ndp):
        dest = lax.rem(d + n, ndp)
        go(rc(crecv.at[:, :, colsl(dest)], cotx.at[0, d], cxs.at[n], cxr.at[n], at_x(n)))
    cotx[0, d] = crecv[:, :, colsl(d)]
    go(rc(cotx.at[0, d], cotx.at[1, d], cds.at[0], cdr.at[0], partner))

    combine(0)
    out0 = pltpu.make_async_copy(obuf.at[0], out.at[0], lsem.at[6])
    out0.start()

    @pl.when(s > 0)
    def _():
        for r in range(ndp):
            cs = colsl(lax.rem(d + (0, 1, 3, 2)[r], ndp))
            rc(xin.at[1, :, cs], xin.at[1, :, cs], zss.at[r], zrs.at[r], (s - 1, i, d)).wait_recv()

    @pl.when(s == 0)
    def _():
        l_fresh.wait()

    dispatch(1)

    for n in range(1, ndp):
        x = lax.rem(d + ndp - n, ndp)
        rc(cotx.at[0, x], cotx.at[0, x], cxs.at[n], cxr.at[n], at_x(n)).wait_recv()
        go(rc(cotx.at[0, x], cotx.at[1, x], cds.at[n], cdr.at[n], partner))
    spread(1)

    def grad(k):
        for n in range(ndp):
            x = lax.rem(d + ndp - n, ndp)
            if k == 0:
                rc(cotx.at[1, x], cotx.at[1, x], cds.at[n], cdr.at[n], partner).wait_recv()
            if n > 0:
                rc(hid.at[k, x], hid.at[k, x], hss.at[k, n], hrs.at[k, n], at_x(n)).wait_recv()
            cr = cotx[:, x, :, pl.ds(k * SLOTS, SLOTS), :].reshape(nexp * SLOTS, cols)
            add = jnp.dot(hid[k, x], cr, preferred_element_type=F32)
            if k == 0 and n == 0:
                gacc[...] = add
            else:
                gacc[...] += add

    wait_spread(1)
    h1 = gate_up(1)
    down(1, h1)
    grad(0)
    grad(1)
    gout = pltpu.make_async_copy(gacc, grad_out, lsem.at[7])
    gout.start()
    combine(1)
    out1 = pltpu.make_async_copy(obuf.at[1], out.at[1], lsem.at[8])
    out1.start()
    for cp in sends:
        cp.wait_send()

    @pl.when(s < nsec - 1)
    def _():
        for r in range(ndp):
            cs = colsl(lax.rem(d + (0, 1, 3, 2)[r], ndp))
            rc(obuf.at[0, :, cs], xin.at[1, :, cs], zss.at[r], zrs.at[r], (s + 1, i, d)).wait_send()

    out0.wait()
    gout.wait()
    out1.wait()


def local(nsec, nexp, ndp, arrivals, fresh, routes, gates, cotangent, norm_gain, w_gate, w_up, w_down):
    tok, width = arrivals.shape[1:]
    hidn, cols = w_gate.shape[1:]
    flight = nexp // SPLIT
    ny = nexp // 2
    steps = routes.shape[1]
    rows = nexp * SLOTS
    routes_t = jnp.transpose(routes[0], (0, 2, 1))
    gates_t = jnp.transpose(gates[0], (0, 2, 1)).astype(F32)
    any_spec = pl.BlockSpec(memory_space=pl.ANY)
    vm_spec = pl.BlockSpec(memory_space=pltpu.VMEM)
    dma = pltpu.SemaphoreType.DMA
    out, grad = pl.pallas_call(
        functools.partial(kernel_body, nsec, nexp, ndp),
        name="moe_relay",
        out_shape=(
            jax.ShapeDtypeStruct((steps, tok, width), BF16),
            jax.ShapeDtypeStruct((hidn, cols), F32),
        ),
        in_specs=[any_spec, any_spec, vm_spec, vm_spec, any_spec, vm_spec, any_spec, any_spec, any_spec],
        out_specs=(any_spec, any_spec),
        scratch_shapes=[
            pltpu.VMEM((2, tok, width), BF16),
            pltpu.VMEM((2, tok, width), BF16),
            pltpu.VMEM((3, hidn, width), BF16),
            pltpu.VMEM((2, flight, SLOTS, width), BF16),
            pltpu.VMEM((2, 2, ny, SLOTS, width), BF16),
            pltpu.VMEM((flight, 2 * SLOTS, width), BF16),
            pltpu.VMEM((ny, 2 * SLOTS, width), BF16),
            pltpu.VMEM((2, ndp, ny, 2 * SLOTS, cols), BF16),
            pltpu.VMEM((2, ndp, hidn, rows), BF16),
            pltpu.VMEM((2, ndp, rows // 2, cols), BF16),
            pltpu.VMEM((2, ndp, rows // 2, cols), BF16),
            pltpu.VMEM((2, ndp, ny, SLOTS, cols), BF16),
            pltpu.VMEM((2, ndp, ny, SLOTS, cols), BF16),
            pltpu.VMEM((2, tok, ny * SLOTS), BF16),
            pltpu.VMEM((2, tok, width), BF16),
            pltpu.VMEM((hidn, cols), F32),
            dma((9,)),
            dma((3, 2)), dma((3, 2)), dma((3, 2)), dma((3, 2)),
            dma((2, ny)), dma((2, ny)), dma((2, ny)), dma((2, ny)),
            dma((ny,)), dma((ny,)), dma((ndp,)), dma((ndp,)), dma((ndp,)), dma((ndp,)),
            dma((2, ndp)), dma((2, ndp)), dma((2, ndp)), dma((2, ndp)),
            dma((2, ndp, ny)), dma((2, ndp, ny)), dma((ndp,)), dma((ndp,)),
        ],
        compiler_params=pltpu.CompilerParams(
            collective_id=0, has_side_effects=True, vmem_limit_bytes=60 * 1024 * 1024
        ),
    )(
        arrivals[0], fresh[0], routes_t, gates_t, cotangent[0], norm_gain, w_gate[0], w_up[0], w_down[0]
    )
    return out[None], grad[None]


def solution(mesh):
    placed = (
        P("section", ("expert", "dp"), None),
        P(None, ("expert", "dp"), None),
        P("section", None, ("expert", "dp"), None),
        P("section", None, ("expert", "dp"), None),
        P("section", None, ("expert", "dp"), None),
        P("section", None),
        P("section", "expert", "dp"),
        P("section", "expert", "dp"),
        P("section", "expert", "dp"),
    )
    return jax.shard_map(
        functools.partial(local, mesh.shape["section"], mesh.shape["expert"], mesh.shape["dp"]),
        mesh=mesh,
        in_specs=placed,
        out_specs=(P("section", None, ("expert", "dp"), None), P("section", "expert", "dp")),
        check_vma=False,
    )
```

time: 259 us -> 106 us (0.41)
  the two profiles are of different devices: /device:TPU:1 before, /device:TPU:256 now
where the time goes in v1:
time: 106 us; the launch traced here: 105 us
  Pallas kernels  100 us (94%)
  local copies, waits for them, and re-layouts  4.19 us (4%)
    pallas_call x1, Pallas kernels, local(): pl.pallas_call(functools.partial(kernel_body, nsec, nexp, ndp), name='moe...  100 us
    unnamed x9, local copies, waits for them, and re-layouts  4.19 us

profile of v1, /device:TPU:256, one launch (start us, length us, event | category | flops | bytes accessed | tf_op | source)
XLA Modules:
  0.0 105.4 jit_solution(11409248848343092352)
XLA Ops:
  0.6 0.0 copy-start.1
  0.6 0.7 copy-done.1
  1.3 0.0 copy-start.2
  1.3 0.6 copy.15
  1.9 0.1 copy-done.2
  2.0 0.6 convert_bitcast_fusion.gates
  2.6 100.0 %moe_relay.1 = (bf16[2,64,2048]{2,1,0:T(8,128)(2,1)}, f32[352,512]{1,0:T(8,128)}) custom-call(bf16[64,2048]{1,0:T(8,128)(2,1)} %bitcast.24, bf16[64,2048]{1,0:T(8,128)(2,1)} %bitcast.25, s32[2,6,64]{2,1,0:T(8,128)} %bitcast.26, f32[2,6,64]{2,1,0:T(8,128)} %convert_bitcast_fusion.gates, bf16[2,64,2048]{2,1,0:T(8,128)(2,1)} %bitcast.20, f32[1,2048]{1,0:T(1,128)} %gain.1, ...), custom_call_target="tpu_custom_call" | custom-call | tf_op jit(solution)/shard_map/moe_relay/pallas_call | solution.py:332
  102.6 0.0 copy-start
  102.6 1.9 %copy.18 = bf16[1,2,64,2048]{3,2,1,0:T(8,128)(2,1)} copy(bf16[1,2,64,2048]{3,2,1,0:T(8,128)(2,1)} %bitcast.19) | data formatting | bytes 1048576
  104.6 0.0 copy-done
  104.6 0.9 copy.19
Async XLA Ops:
  0.6 0.7 copy-start.1
  1.3 0.7 copy-start.2
  102.6 2.0 %copy-start = (f32[352,512]{1,0:T(8,128)S(1)}, f32[352,512]{1,0:T(8,128)}, u32[]{:S(2)}) copy-start(f32[352,512]{1,0:T(8,128)} %get-tuple-element.5) | copy-start | bytes 2162692

commit v2 on v1

--- a/solution.py
+++ b/solution.py
@@ -10,6 +10,7 @@
 SPLIT = 4
 CAP = 12
 SLOTS = 16
+NEAR = (3, 5, 2, 6, 1, 7)
 MESH = pl.DeviceIdType.MESH
 NT = (((1,), (1,)), ((), ()))
 TN = (((0,), (0,)), ((), ()))
@@ -21,10 +22,10 @@
     nsec, nexp, ndp,
     arr, fresh, routes, gates, cot, gain, wg, wu, wd,
     out, grad_out,
-    xin, cin, wbuf, tsend, trecv, csend, crecv, cotx, hid, dsend, drecv, rsend, rrecv,
-    mix, obuf, gacc,
+    xin, cin, wbuf, tsend, trecv, csend, crecv, cotx, hid, dsend, drecv, psum, rsend, mrecv, rrecv,
+    rts, gts, selb, selg, mix, mixs, obuf, gacc,
     lsem, wss, wrs, fss, frs, tss, trs, tds, tdr, css, crs, cxs, cxr, cds, cdr,
-    hss, hrs, dss, drs, rss, rrs, zss, zrs,
+    hss, hrs, dss, drs, mss, mrs, rss, rrs, zss, zrs,
 ):
     s = lax.axis_index("section")
     i = lax.axis_index("expert")
@@ -35,6 +36,17 @@
     tok, width = arr.shape
     hidn, cols = wg.shape
     half = hidn // 2
+    wide = tsend.shape[3]
+    step = wide // 3
+    rwide = rsend.shape[4]
+    rstep = rwide // 3
+    far = ny // 2
+    near = [n for n in NEAR if 0 < n < ny and n != far]
+    odd = lax.rem(y, 2)
+    mate = y + 1 - 2 * odd
+    mate_far = lax.rem(mate + far, ny)
+    relay_n = far - 1 + 2 * odd
+    mate_dev = (s, mate * 2 + c, d)
     flight = nexp // SPLIT
     rows = flight * SLOTS
 
@@ -71,6 +83,10 @@
         for m, w in enumerate((wg, wu, wd))
     ]
     l_fresh = pltpu.make_async_copy(fresh, xin.at[1], lsem.at[5])
+    l_rt = pltpu.make_async_copy(routes, rts, lsem.at[9])
+    l_gt = pltpu.make_async_copy(gates, gts, lsem.at[10])
+    l_rt.start()
+    l_gt.start()
     l_arr.start()
     for l in l_w:
         l.start()
@@ -81,7 +97,7 @@
         l_fresh.start()
 
     bar = pltpu.get_barrier_semaphore()
-    peers = [at_x(k) for k in range(1, ndp)] + [at_y(k) for k in range(1, ny)] + [partner]
+    peers = [at_x(k) for k in range(1, ndp)] + [at_y(n) for n in near] + [partner]
     for p in peers:
         pl.semaphore_signal(bar, inc=1, device_id=p, device_id_type=MESH)
 
@@ -93,15 +109,22 @@
     def _():
         pl.semaphore_signal(bar, inc=1, device_id=(s + 1, i, d), device_id_type=MESH)
 
-    slot = lax.rem(lax.broadcasted_iota(jnp.int32, (rows, tok), 0), SLOTS)
+    pos = lax.rem(lax.broadcasted_iota(jnp.int32, (rows, tok), 0), SLOTS)
+    tail = SLOTS - CAP
+    maps = [jnp.where(pos < CAP, pos, -5).astype(F32)]
+    for q in range(3):
+        maps.append(jnp.where(pos >= CAP, pos - CAP + tail * q, -5).astype(F32))
     ia = lax.broadcasted_iota(jnp.int32, (tok, tok), 0)
     ib = lax.broadcasted_iota(jnp.int32, (tok, tok), 1)
     before = (ia < ib).astype(F32).astype(BF16)
     eye = (ia == ib).astype(F32).astype(BF16)
-    sels, selgs = [], []
+    l_rt.wait()
+    l_gt.wait()
+    rt = rts[...]
+    gt = gts[...].astype(F32)
     for k in range(2):
-        r = routes[k]
-        g = gates[k]
+        r = rt[:, k, :]
+        g = gt[:, k, :]
         names, shares = [], []
         for e in range(flight):
             m = r == e
@@ -112,30 +135,47 @@
         naming = jnp.concatenate(names, axis=0)
         share = jnp.concatenate(shares, axis=0)
         places = jnp.dot(naming.astype(BF16), before, preferred_element_type=F32)
-        chosen = (naming > 0.5) & (jnp.abs(places - slot.astype(F32)) < 0.5) & (slot < CAP)
-        sel = jnp.where(chosen, 1.0, 0.0).astype(BF16)
-        selg = jnp.where(chosen, share, 0.0).astype(BF16)
-        sels.append(sel)
-        selgs.append(selg)
-        g3 = selg.reshape(flight, 1, SLOTS, tok)
-        g3 = jnp.concatenate([g3, g3], axis=1).reshape(2 * rows, tok)
-        mix[k] = lax.dot_general(eye, g3, NT, preferred_element_type=F32).astype(BF16)
+        picks, mixes = [], []
+        for slot in maps:
+            chosen = (naming > 0.5) & (jnp.abs(places - slot) < 0.5)
+            picks.append(jnp.where(chosen, 1.0, 0.0).astype(BF16))
+            g3 = jnp.where(chosen, share, 0.0).astype(BF16)
+            if not mixes:
+                selg[k] = g3
+            g3 = g3.reshape(flight, 1, SLOTS, tok)
+            g3 = jnp.concatenate([g3, g3], axis=1).reshape(2 * rows, tok)
+            mixes.append(lax.dot_general(eye, g3, NT, preferred_element_type=F32).astype(BF16))
+        mix[k] = mixes[0]
+        mixs[k] = jnp.concatenate(mixes[1:], axis=1)
+        for q in range(3):
+            selb[k, q] = jnp.concatenate([picks[0], picks[q + 1]], axis=1)
+        for r in range(ndp):
+            rrecv[k, r, lax.rem(y + far, ny)] = jnp.zeros((SLOTS, rwide), BF16)
 
     pl.semaphore_wait(
         bar,
         len(peers) + jnp.where(s > 0, 1, 0) + jnp.where(s < nsec - 1, 1, 0),
     )
 
+    def part_of(w, j, own):
+        return w.at[pl.ds(j * half, half), colsl(own)] if own is not None else w.at[pl.ds(j * half, half)]
+
     def send_w(m, w):
+        for q in range(2):
+            for j, k in enumerate((1, ndp - 1)):
+                p = j if q == 0 else 1 - j
+                go(rc(part_of(w, p, None), part_of(wbuf.at[m], p, d), wss.at[m, j, q], wrs.at[m, j, q], at_x(k)))
+
+    def forward_w(m):
         for j, k in enumerate((1, ndp - 1)):
-            go(rc(w, wbuf.at[m, :, colsl(d)], wss.at[m, j], wrs.at[m, j], at_x(k)))
-
-    def forward_w(m, w):
+            part = part_of(wbuf.at[m], j, lax.rem(d + ndp - k, ndp))
+            rc(part, part, wss.at[m, j, 0], wrs.at[m, j, 0], at_x(k)).wait_recv()
+            go(rc(part, part, fss.at[m, j], frs.at[m, j], at_x(k)))
+
+    def wait_near(m):
         for j, k in enumerate((1, ndp - 1)):
-            owner = lax.rem(d + ndp - k, ndp)
-            rc(w, wbuf.at[m, :, colsl(owner)], wss.at[m, j], wrs.at[m, j], at_x(k)).wait_recv()
-            part = wbuf.at[m, pl.ds(j * half, half), colsl(owner)]
-            go(rc(part, part, fss.at[m, j], frs.at[m, j], at_x(k)))
+            part = part_of(wbuf.at[m], 1 - j, lax.rem(d + ndp - k, ndp))
+            rc(part, part, wss.at[m, j, 1], wrs.at[m, j, 1], at_x(k)).wait_recv()
 
     def wait_far(m):
         owner = lax.rem(d + 2, ndp)
@@ -152,88 +192,169 @@
         x = xin[k].astype(F32)
         scale = lax.rsqrt(jnp.mean(x * x, axis=1, keepdims=True) + 0.5)
         normed = (x * scale * gains).astype(BF16)
-        picked = jnp.dot(sels[k], normed, preferred_element_type=F32).astype(BF16)
-        tsend[k] = picked.reshape(flight, SLOTS, width)
+        last = normed[:, wide:]
+        for q in range(3):
+            both = jnp.concatenate([normed[:, q * step : (q + 1) * step], last], axis=0)
+            picked = jnp.dot(selb[k, q], both, preferred_element_type=F32).astype(BF16)
+            tsend[k, :, :, q * step : (q + 1) * step] = picked.reshape(flight, SLOTS, step)
         own = tsend.at[k, lax.div(y, 2)]
-        for n in range(1, ny):
+        for n in near:
             dest = lax.rem(y + n, ny)
             go(rc(tsend.at[k, lax.div(dest, 2)], trecv.at[k, 0, y], tss.at[k, n], trs.at[k, n], at_y(n)))
         go(rc(own, trecv.at[k, 1, y], tds.at[k, 0], tdr.at[k, 0], partner))
         trecv[k, 0, y] = tsend[k, lax.div(y, 2)]
 
     def spread(k):
-        for n in range(1, ny):
+        blk = trecv.at[k, 0, mate_far]
+        rc(blk, blk, tss.at[k, relay_n], trs.at[k, relay_n], mate_dev).wait_recv()
+        go(rc(blk, blk, tss.at[k, far], trs.at[k, far], mate_dev))
+        go(rc(blk, trecv.at[k, 1, mate_far], tds.at[k, relay_n], tdr.at[k, relay_n], partner))
+        for n in near[::-1]:
             blk = trecv.at[k, 0, ysrc(n)]
-            rc(blk, blk, tss.at[k, n], trs.at[k, n], at_y(n)).wait_recv()
-            go(rc(blk, trecv.at[k, 1, ysrc(n)], tds.at[k, n], tdr.at[k, n], partner))
+            if n in (far - 1, far + 1):
+                @pl.when(relay_n != n)
+                def _(n=n, blk=blk):
+                    rc(blk, blk, tss.at[k, n], trs.at[k, n], at_y(n)).wait_recv()
+                    rc(blk, trecv.at[k, 1, ysrc(n)], tds.at[k, n], tdr.at[k, n], partner).start()
+            else:
+                rc(blk, blk, tss.at[k, n], trs.at[k, n], at_y(n)).wait_recv()
+                go(rc(blk, trecv.at[k, 1, ysrc(n)], tds.at[k, n], tdr.at[k, n], partner))
+        blk = trecv.at[k, 0, ysrc(far)]
+        rc(blk, blk, tss.at[k, far], trs.at[k, far], mate_dev).wait_recv()
+        go(rc(blk, trecv.at[k, 1, ysrc(far)], tds.at[k, far], tdr.at[k, far], partner))
+
+    late = []
+
     def wait_spread(k):
         for n in range(ny):
             blk = trecv.at[k, 1, ysrc(n)]
             rc(blk, blk, tds.at[k, n], tdr.at[k, n], partner).wait_recv()
+        other = 2 * far - relay_n
+        blk = trecv.at[k, 0, ysrc(other)]
+        late.append(rc(blk, blk, tds.at[k, other], tdr.at[k, other], partner))
 
     l_arr.wait()
     dispatch(0)
 
     l_cot.wait()
     for k in range(2):
-        picked = jnp.dot(selgs[k], cin[k], preferred_element_type=F32).astype(BF16)
+        picked = jnp.dot(selg[k], cin[k], preferred_element_type=F32).astype(BF16)
         csend[:, pl.ds(k * SLOTS, SLOTS), :] = picked.reshape(flight, SLOTS, width)
-    for n in range(1, ny):
+    for n in near:
         dest = lax.rem(y + n, ny)
         go(rc(csend.at[lax.div(dest, 2)], crecv.at[y], css.at[n], crs.at[n], at_y(n)))
     crecv[y] = csend[lax.div(y, 2)]
 
-    forward_w(0, wg)
     spread(0)
-    forward_w(1, wu)
+    forward_w(0)
+    forward_w(1)
     send_w(2, wd)
+    blk = crecv.at[mate_far]
+    rc(blk, blk, css.at[relay_n], crs.at[relay_n], mate_dev).wait_recv()
+    go(rc(blk, blk, css.at[far], crs.at[far], mate_dev))
     wait_spread(0)
 
     def gate_up(k):
-        x = trecv[k].reshape(nexp * SLOTS, width)
+        count = nexp * SLOTS
+        pieces = [trecv[k, :, :, :, q * step : (q + 1) * step].reshape(count, step) for q in range(3)]
+        tails = [trecv[k, :, :, 8:, q * step : (q + 1) * step].astype(F32).reshape(count // 2, step) for q in range(3)]
+        low = lax.rem(lax.broadcasted_iota(jnp.int32, (count // 2, step), 0), 8) < 4
+        first = jnp.where(low, turned(tails[0]), tails[1])
+        second = turned(tails[2])
+        merged = jnp.concatenate(
+            [first.reshape(nexp, 1, 8, step), second.reshape(nexp, 1, 8, step)], axis=1
+        ).reshape(count, step)
+        x = jnp.concatenate(pieces + [merged.astype(BF16)], axis=1)
         ga = lax.dot_general(wbuf[0], x, NT, preferred_element_type=F32)
         ua = lax.dot_general(wbuf[1], x, NT, preferred_element_type=F32)
         h = (ga / (1.0 + jnp.exp(-ga)) * ua).astype(BF16)
         hid[k, d] = h
+        return h
+
+    def turned(v):
+        n, w = v.shape
+        return pltpu.roll(v.reshape(n // 8, 8, w), 4, 1).reshape(n, w)
+
+    def share_hidden(k):
         for n in range(1, ndp):
             go(rc(hid.at[k, d], hid.at[k, d], hss.at[k, n], hrs.at[k, n], at_x(n)))
-        return h
 
     def down(k, h):
         hrows = nexp * SLOTS // 2
 
+        def direct(r, n, dest):
+            return rc(rsend.at[k, r, dest], rrecv.at[k, r, y], rss.at[k, r, n], rrs.at[k, r, n], at_y(n))
+
         def finish(r):
             rc(dsend.at[k, r], drecv.at[k, r], dss.at[k, r], drs.at[k, r], partner).wait_recv()
-            total = (rsend[k, r].reshape(hrows, cols).astype(F32) + drecv[k, r].astype(F32)).astype(BF16)
-            rsend[k, r] = total.reshape(ny, SLOTS, cols)
-            for n in range(1, ny):
-                go(rc(rsend.at[k, r, lax.rem(y + n, ny)], rrecv.at[k, r, y], rss.at[k, r, n], rrs.at[k, r, n], at_y(n)))
+            total = psum[r] + drecv[k, r].astype(F32)
+            t4 = total.reshape(ny, 2, 8, cols)
+            lo, hi = t4[:, 0].reshape(ny * 8, cols), t4[:, 1].reshape(ny * 8, cols)
+            lo3, hi3 = lo[:, rwide:], hi[:, rwide:]
+            fill = jnp.concatenate([turned(lo3), lo3, turned(hi3)], axis=1)
+            low = lax.rem(lax.broadcasted_iota(jnp.int32, (ny * 8, rwide), 0), 8) < 4
+            hi = jnp.where(low, hi[:, :rwide], fill)
+            packed = jnp.concatenate(
+                [lo[:, :rwide].reshape(ny, 1, 8, rwide), hi.reshape(ny, 1, 8, rwide)], axis=1
+            )
+            rsend[k, r] = packed.reshape(ny, SLOTS, rwide).astype(BF16)
+            go(rc(rsend.at[k, r, lax.rem(y + far, ny)], mrecv.at[k, r], mss.at[k, r], mrs.at[k, r], mate_dev))
+            for n in near:
+                if n in (far - 1, far + 1):
+                    @pl.when(2 * far - relay_n != n)
+                    def _(n=n):
+                        direct(r, n, lax.rem(y + n, ny)).start()
+                else:
+                    go(direct(r, n, lax.rem(y + n, ny)))
             rrecv[k, r, y] = rsend[k, r, y]
+
+        def finish_far(r):
+            rc(mrecv.at[k, r], mrecv.at[k, r], mss.at[k, r], mrs.at[k, r], mate_dev).wait_recv()
+            both = rsend[k, r, mate_far].astype(F32) + mrecv[k, r].astype(F32)
+            rsend[k, r, mate_far] = both.astype(BF16)
+            n = 2 * far - relay_n
+            dest = (s, mate_far * 2 + c, d)
+            rc(rsend.at[k, r, mate_far], rrecv.at[k, r, y], rss.at[k, r, n], rrs.at[k, r, n], dest).start()
+            for n in (far - 1, far + 1):
+                late.append(direct(r, n, lax.rem(y + n, ny)))
 
         for r in range(ndp):
             if k == 0 and r == 1:
-                forward_w(2, wd)
+                forward_w(2)
+                share_hidden(0)
+                wait_near(2)
             if k == 0 and r == 3:
                 wait_far(2)
             off = (0, 1, 3, 2)[r]
             x = lax.rem(d + off, ndp)
-            part = lax.dot_general(h, wbuf[2, :, colsl(x)], TN, preferred_element_type=F32).astype(BF16)
-            dsend[k, r] = part[hrows:]
+            part = lax.dot_general(h, wbuf[2, :, colsl(x)], TN, preferred_element_type=F32)
+            dsend[k, r] = part[hrows:].astype(BF16)
             go(rc(dsend.at[k, r], drecv.at[k, r], dss.at[k, r], drs.at[k, r], partner))
-            rsend[k, r] = part[:hrows].reshape(ny, SLOTS, cols)
+            psum[r] = part[:hrows]
             if r > 0:
                 finish(r - 1)
+            if r > 1:
+                finish_far(r - 2)
         finish(ndp - 1)
+        finish_far(ndp - 2)
+        finish_far(ndp - 1)
 
     def combine(k):
         for r in range(ndp):
             off = (0, 1, 3, 2)[r]
             cs = colsl(lax.rem(d + off, ndp))
-            for n in range(1, ny):
+            for n in near[::-1]:
                 blk = rrecv.at[k, r, ysrc(n)]
                 rc(blk, blk, rss.at[k, r, n], rrs.at[k, r, n], at_y(n)).wait_recv()
-            got = rrecv[k, r].reshape(ny * SLOTS, cols)
-            res = xin[k, :, cs].astype(F32) + jnp.dot(mix[k], got, preferred_element_type=F32)
+            got = rrecv[k, r].reshape(ny * SLOTS, rwide)
+            folded = jnp.concatenate([got[:, q * rstep : (q + 1) * rstep] for q in range(3)], axis=0)
+            res = xin[k, :, cs].astype(F32) + jnp.concatenate(
+                [
+                    jnp.dot(mix[k], got, preferred_element_type=F32),
+                    jnp.dot(mixs[k], folded, preferred_element_type=F32),
+                ],
+                axis=1,
+            )
             obuf[k, :, cs] = res.astype(BF16)
             if k == 0:
                 @pl.when(s < nsec - 1)
@@ -242,15 +363,25 @@
 
     l_w[0].wait()
     l_w[1].wait()
+    wait_near(0)
+    wait_near(1)
     wait_far(0)
     wait_far(1)
     h0 = gate_up(0)
     l_w[2].wait()
     down(0, h0)
 
-    for n in range(1, ny):
-        blk = crecv.at[ysrc(n)]
-        rc(blk, blk, css.at[n], crs.at[n], at_y(n)).wait_recv()
+    for n in near:
+        if n in (far - 1, far + 1):
+            @pl.when(relay_n != n)
+            def _(n=n):
+                blk = crecv.at[ysrc(n)]
+                rc(blk, blk, css.at[n], crs.at[n], at_y(n)).wait_recv()
+        else:
+            blk = crecv.at[ysrc(n)]
+            rc(blk, blk, css.at[n], crs.at[n], at_y(n)).wait_recv()
+    blk = crecv.at[ysrc(far)]
+    rc(blk, blk, css.at[far], crs.at[far], mate_dev).wait_recv()
     for n in range(1, ndp):
         dest = lax.rem(d + n, ndp)
         go(rc(crecv.at[:, :, colsl(dest)], cotx.at[0, d], cxs.at[n], cxr.at[n], at_x(n)))
@@ -295,6 +426,7 @@
 
     wait_spread(1)
     h1 = gate_up(1)
+    share_hidden(1)
     down(1, h1)
     grad(0)
     grad(1)
@@ -303,7 +435,7 @@
     combine(1)
     out1 = pltpu.make_async_copy(obuf.at[1], out.at[1], lsem.at[8])
     out1.start()
-    for cp in sends:
+    for cp in sends + late:
         cp.wait_send()
 
     @pl.when(s < nsec - 1)
@@ -324,8 +456,10 @@
     ny = nexp // 2
     steps = routes.shape[1]
     rows = nexp * SLOTS
-    routes_t = jnp.transpose(routes[0], (0, 2, 1))
-    gates_t = jnp.transpose(gates[0], (0, 2, 1)).astype(F32)
+    routes_t = jnp.transpose(routes[0], (2, 0, 1))
+    gates_t = jnp.transpose(gates[0], (2, 0, 1))
+    wide = width // 4 * 3
+    rwide = cols // 4 * 3
     any_spec = pl.BlockSpec(memory_space=pl.ANY)
     vm_spec = pl.BlockSpec(memory_space=pltpu.VMEM)
     dma = pltpu.SemaphoreType.DMA
@@ -336,30 +470,37 @@
             jax.ShapeDtypeStruct((steps, tok, width), BF16),
             jax.ShapeDtypeStruct((hidn, cols), F32),
         ),
-        in_specs=[any_spec, any_spec, vm_spec, vm_spec, any_spec, vm_spec, any_spec, any_spec, any_spec],
+        in_specs=[any_spec, any_spec, any_spec, any_spec, any_spec, vm_spec, any_spec, any_spec, any_spec],
         out_specs=(any_spec, any_spec),
         scratch_shapes=[
             pltpu.VMEM((2, tok, width), BF16),
             pltpu.VMEM((2, tok, width), BF16),
             pltpu.VMEM((3, hidn, width), BF16),
-            pltpu.VMEM((2, flight, SLOTS, width), BF16),
-            pltpu.VMEM((2, 2, ny, SLOTS, width), BF16),
+            pltpu.VMEM((2, flight, SLOTS, wide), BF16),
+            pltpu.VMEM((2, 2, ny, SLOTS, wide), BF16),
             pltpu.VMEM((flight, 2 * SLOTS, width), BF16),
             pltpu.VMEM((ny, 2 * SLOTS, width), BF16),
             pltpu.VMEM((2, ndp, ny, 2 * SLOTS, cols), BF16),
             pltpu.VMEM((2, ndp, hidn, rows), BF16),
             pltpu.VMEM((2, ndp, rows // 2, cols), BF16),
             pltpu.VMEM((2, ndp, rows // 2, cols), BF16),
-            pltpu.VMEM((2, ndp, ny, SLOTS, cols), BF16),
-            pltpu.VMEM((2, ndp, ny, SLOTS, cols), BF16),
+            pltpu.VMEM((ndp, rows // 2, cols), F32),
+            pltpu.VMEM((2, ndp, ny, SLOTS, rwide), BF16),
+            pltpu.VMEM((2, ndp, SLOTS, rwide), BF16),
+            pltpu.VMEM((2, ndp, ny, SLOTS, rwide), BF16),
+            pltpu.VMEM(routes_t.shape, jnp.int32),
+            pltpu.VMEM(gates_t.shape, BF16),
+            pltpu.VMEM((2, 3, flight * SLOTS, 2 * tok), BF16),
+            pltpu.VMEM((2, flight * SLOTS, tok), BF16),
             pltpu.VMEM((2, tok, ny * SLOTS), BF16),
+            pltpu.VMEM((2, tok, 3 * ny * SLOTS), BF16),
             pltpu.VMEM((2, tok, width), BF16),
             pltpu.VMEM((hidn, cols), F32),
-            dma((9,)),
-            dma((3, 2)), dma((3, 2)), dma((3, 2)), dma((3, 2)),
+            dma((11,)),
+            dma((3, 2, 2)), dma((3, 2, 2)), dma((3, 2)), dma((3, 2)),
             dma((2, ny)), dma((2, ny)), dma((2, ny)), dma((2, ny)),
             dma((ny,)), dma((ny,)), dma((ndp,)), dma((ndp,)), dma((ndp,)), dma((ndp,)),
-            dma((2, ndp)), dma((2, ndp)), dma((2, ndp)), dma((2, ndp)),
+            dma((2, ndp)), dma((2, ndp)), dma((2, ndp)), dma((2, ndp)), dma((2, ndp)), dma((2, ndp)),
             dma((2, ndp, ny)), dma((2, ndp, ny)), dma((ndp,)), dma((ndp,)),
         ],
         compiler_params=pltpu.CompilerParams(

time: 106 us -> 103 us (0.972)
  the two profiles are of different devices: /device:TPU:256 before, /device:TPU:1 now
where the time goes in v2:
time: 103 us; the launch traced here: 102 us
  Pallas kernels  98.8 us (96%)
  local copies, waits for them, and re-layouts  2.81 us (3%)
    pallas_call x1, Pallas kernels, local(): pl.pallas_call(functools.partial(kernel_body, nsec, nexp, ndp), name='moe...  98.8 us
    unnamed x4, local copies, waits for them, and re-layouts  2.81 us

profile of v2, /device:TPU:1, one launch (start us, length us, event | category | flops | bytes accessed | tf_op | source)
XLA Modules:
  0.0 102.3 jit_solution(151693279238387712)
XLA Ops:
  0.6 98.8 %moe_relay.1 = (bf16[2,64,2048]{2,1,0:T(8,128)(2,1)}, f32[352,512]{1,0:T(8,128)}) custom-call(bf16[64,2048]{1,0:T(8,128)(2,1)} %bitcast.20, bf16[64,2048]{1,0:T(8,128)(2,1)} %bitcast.21, s32[6,2,64]{2,1,0:T(2,128)} %bitcast.22, bf16[6,2,64]{2,1,0:T(2,128)(2,1)} %bitcast.23, bf16[2,64,2048]{2,1,0:T(8,128)(2,1)} %bitcast.16, f32[1,2048]{1,0:T(1,128)} %gain.1, ...), custom_call_target="tpu_custom_call" | custom-call | tf_op jit(solution)/shard_map/moe_relay/pallas_call | solution.py:466
  99.5 0.0 copy-start
  99.5 1.9 %copy.13 = bf16[1,2,64,2048]{3,2,1,0:T(8,128)(2,1)} copy(bf16[1,2,64,2048]{3,2,1,0:T(8,128)(2,1)} %bitcast.15) | data formatting | bytes 1048576
  101.5 0.0 copy-done
  101.5 0.9 copy.14
Async XLA Ops:
  99.5 2.0 %copy-start = (f32[352,512]{1,0:T(8,128)S(1)}, f32[352,512]{1,0:T(8,128)}, u32[]{:S(2)}) copy-start(f32[352,512]{1,0:T(8,128)} %get-tuple-element.5) | copy-start | bytes 2162692

commit v3 on v1

v3 whole, which is shorter than its diff:
```python
import functools

import jax
import jax.numpy as jnp
from jax import lax
from jax.experimental import pallas as pl
from jax.experimental.pallas import tpu as pltpu
from jax.sharding import PartitionSpec as P

SPLIT = 4
CAP = 12
SLOTS = 16
NEAR = (3, 5, 2, 6, 1, 7)
ORDER = (0, 1, 3, 2)
MESH = pl.DeviceIdType.MESH
NT = (((1,), (1,)), ((), ()))
TN = (((0,), (0,)), ((), ()))
F32 = jnp.float32
BF16 = jnp.bfloat16


def kernel_body(
    nsec, nexp, ndp,
    arr, fresh, routes, gates, cot, gain, wg, wu, wd,
    out, grad_out,
    xin, cin, wbuf, tsend, trecv, xraw, csend, crecv, cstage, cotx, hid, dsend, drecv, psum, rsend, mrecv, rrecv,
    rts, gts, gns, selb, selgb, mix, mixs, obuf, gacc,
    lsem, sends, wrs, wns, frs, trs, tdr, crs, cxr, cgr, cfr, cdr, hrs, hns, hfr, drs, mrs, rrs, zrs,
):
    s = lax.axis_index("section")
    i = lax.axis_index("expert")
    d = lax.axis_index("dp")
    ny = nexp // 2
    y = lax.div(i, 2)
    c = lax.rem(i, 2)
    tok, width = arr.shape
    hidn, cols = wg.shape
    half = hidn // 2
    rwide = rsend.shape[4]
    rstep = rwide // 3
    far = ny // 2
    near = [n for n in NEAR if 0 < n < ny and n != far]
    odd = lax.rem(y, 2)
    mate = y + 1 - 2 * odd
    mate_far = lax.rem(mate + far, ny)
    relay_n = far - 1 + 2 * odd
    mate_dev = (s, mate * 2 + c, d)
    flight = nexp // SPLIT
    rows = flight * SLOTS

    def at_x(k):
        return (s, i, lax.rem(d + k, ndp))

    def at_y(k):
        return (s, lax.rem(y + k, ny) * 2 + c, d)

    def ysrc(k):
        return lax.rem(y + ny - k, ny)

    partner = (s, y * 2 + 1 - c, d)

    def colsl(x):
        return pl.ds(pl.multiple_of(x * cols, cols), cols)

    def rc(src, dst, ss, rs, dev):
        return pltpu.make_async_remote_copy(
            src_ref=src, dst_ref=dst, send_sem=ss, recv_sem=rs, device_id=dev, device_id_type=MESH
        )

    s_w, s_t, s_c, s_x, s_h, s_d, s_m, s_r, s_z = (sends.at[n] for n in range(9))

    def drain(sem, ref):
        rc(ref, ref, sem, sem, partner).wait_send()

    def arrived(sem, ref):
        rc(ref, ref, sem, sem, partner).wait_recv()

    l_arr = pltpu.make_async_copy(arr, xin.at[0], lsem.at[0])
    l_cot = pltpu.make_async_copy(cot, cin, lsem.at[1])
    l_w = [
        pltpu.make_async_copy(w, wbuf.at[m, :, colsl(d)], lsem.at[2 + m])
        for m, w in enumerate((wg, wu, wd))
    ]
    l_fresh = pltpu.make_async_copy(fresh, xin.at[1], lsem.at[5])
    l_rt = pltpu.make_async_copy(routes, rts, lsem.at[9])
    l_gt = pltpu.make_async_copy(gates, gts, lsem.at[10])
    l_gn = pltpu.make_async_copy(gain, gns, lsem.at[11])
    l_gn.start()
    l_rt.start()
    l_gt.start()
    l_arr.start()
    for l in l_w:
        l.start()
    l_cot.start()

    @pl.when(s == 0)
    def _():
        l_fresh.start()

    bar = pltpu.get_barrier_semaphore()
    peers = [at_x(k) for k in range(1, ndp)] + [at_y(n) for n in near] + [partner]
    for p in peers:
        pl.semaphore_signal(bar, inc=1, device_id=p, device_id_type=MESH)

    @pl.when(s > 0)
    def _():
        pl.semaphore_signal(bar, inc=1, device_id=(s - 1, i, d), device_id_type=MESH)

    @pl.when(s < nsec - 1)
    def _():
        pl.semaphore_signal(bar, inc=1, device_id=(s + 1, i, d), device_id_type=MESH)

    with jax.named_scope("bar"):
        pl.semaphore_wait(
            bar,
            len(peers) + jnp.where(s > 0, 1, 0) + jnp.where(s < nsec - 1, 1, 0),
        )

    def part_of(w, j, own):
        return w.at[pl.ds(j * half, half), colsl(own)] if own is not None else w.at[pl.ds(j * half, half)]

    def send_w(m, w):
        for q in range(2):
            for j, k in enumerate((1, ndp - 1)):
                p = j if q == 0 else 1 - j
                rs = wrs.at[m, j] if q == 0 else wns.at[m]
                rc(part_of(w, p, None), part_of(wbuf.at[m], p, d), s_w, rs, at_x(k)).start()

    def forward_w(m):
        for j, k in enumerate((1, ndp - 1)):
            part = part_of(wbuf.at[m], j, lax.rem(d + ndp - k, ndp))
            arrived(wrs.at[m, j], part)
            rc(part, part, s_w, frs.at[m], at_x(k)).start()

    def wait_near(m):
        arrived(wns.at[m], wbuf.at[m, :, pl.ds(0, cols)])

    def wait_far(m):
        arrived(frs.at[m], wbuf.at[m, :, pl.ds(0, cols)])

    send_w(0, wg)
    send_w(1, wu)

    pos = lax.rem(lax.broadcasted_iota(jnp.int32, (rows, tok), 0), SLOTS)
    tail = SLOTS - CAP
    maps = [jnp.where(pos < CAP, pos, -5).astype(F32)]
    for q in range(3):
        maps.append(jnp.where(pos >= CAP, pos - CAP + tail * q, -5).astype(F32))
    ia = lax.broadcasted_iota(jnp.int32, (tok, tok), 0)
    ib = lax.broadcasted_iota(jnp.int32, (tok, tok), 1)
    before = (ia < ib).astype(F32).astype(BF16)
    eye = (ia == ib).astype(F32).astype(BF16)
    l_rt.wait()
    l_gt.wait()
    rt = rts[...]
    gt = gts[...].astype(F32)

    def select(k):
        r = rt[:, k, :]
        g = gt[:, k, :]
        names, shares = [], []
        for e in range(flight):
            m = r == e
            nm = jnp.max(jnp.where(m, 1.0, 0.0), axis=0, keepdims=True)
            sh = jnp.sum(jnp.where(m, g, 0.0), axis=0, keepdims=True)
            names.append(jnp.broadcast_to(nm, (SLOTS, tok)))
            shares.append(jnp.broadcast_to(sh, (SLOTS, tok)))
        naming = jnp.concatenate(names, axis=0)
        share = jnp.concatenate(shares, axis=0)
        places = jnp.dot(naming.astype(BF16), before, preferred_element_type=F32)
        picks, gated, mixes = [], [], []
        for slot in maps:
            chosen = (naming > 0.5) & (jnp.abs(places - slot) < 0.5)
            picks.append(jnp.where(chosen, 1.0, 0.0).astype(BF16))
            g3 = jnp.where(chosen, share, 0.0).astype(BF16)
            gated.append(g3)
            g3 = g3.reshape(flight, 1, SLOTS, tok)
            g3 = jnp.concatenate([g3, g3], axis=1).reshape(2 * rows, tok)
            mixes.append(lax.dot_general(eye, g3, NT, preferred_element_type=F32).astype(BF16))
        mix[k] = mixes[0]
        mixs[k] = jnp.concatenate(mixes[1:], axis=1)
        for q in range(3):
            selb[k, q] = jnp.concatenate([picks[0], picks[q + 1]], axis=1)
            selgb[k, q] = jnp.concatenate([gated[0], gated[q + 1]], axis=1)

    def view(ref, m, *at):
        return ref.at[(0,) + at] if m == 0 else ref.at[(1,) + at + (m - 1,)]

    def block(r):
        return colsl(lax.rem(d + ORDER[r], ndp))

    def pick(sel, k, x, put):
        last = x[:, rwide:]
        for q in range(3):
            both = jnp.concatenate([x[:, q * rstep : (q + 1) * rstep], last], axis=0)
            got = jnp.dot(sel[k, q], both, preferred_element_type=F32).astype(BF16)
            put(pl.ds(q * rstep, rstep), got.reshape(flight, SLOTS, rstep))

    def dispatch(m):
        k = 0 if m == 0 else 1
        for r in range(ndp) if m == 0 else (m - 1,):

            def put(cs, v, r=r):
                tsend[k, :, r, :, cs] = v

            pick(selb, k, xin[k, :, block(r)], put)
        for n in near:
            dest = lax.rem(y + n, ny)
            src = view(tsend, m, lax.div(dest, 2))
            rc(src, view(trecv, m, 0, y), s_t, trs.at[m, n - 1], at_y(n)).start()
        own = view(tsend, m, lax.div(y, 2))
        rc(own, view(trecv, m, 1, y), s_t, tdr.at[m], partner).start()
        if m == 0:
            trecv[0, 0, y] = tsend[0, lax.div(y, 2)]
        else:
            trecv[1, 0, y, m - 1] = tsend[1, lax.div(y, 2), m - 1]

    def onward(m, src, n):
        blk = view(trecv, m, 0, src)
        arrived(trs.at[m, n - 1], blk)
        rc(blk, view(trecv, m, 1, src), s_t, tdr.at[m], partner).start()

    def relay(m):
        onward(m, mate_far, relay_n)
        blk = view(trecv, m, 0, mate_far)
        rc(blk, blk, s_t, trs.at[m, far - 1], mate_dev).start()

    def spread(m):
        for n in near[::-1]:
            if n in (far - 1, far + 1):

                @pl.when(relay_n != n)
                def _(n=n):
                    onward(m, ysrc(n), n)
            else:
                onward(m, ysrc(n), n)
        onward(m, ysrc(far), far)

    def wait_spread(m):
        arrived(tdr.at[m], trecv.at[0, 1] if m == 0 else trecv.at[1, 1, :, m - 1])

    count = nexp * SLOTS

    def turned(v):
        n, w = v.shape
        return pltpu.roll(v.reshape(n // 8, 8, w), 4, 1).reshape(n, w)

    low = lax.rem(lax.broadcasted_iota(jnp.int32, (count // 2, rstep), 0), 8) < 4

    def merge(get):
        tails = [
            get(pl.ds(8, 8), pl.ds(q * rstep, rstep)).astype(F32).reshape(count // 2, rstep) for q in range(3)
        ]
        first = jnp.where(low, turned(tails[0]), tails[1])
        second = turned(tails[2])
        return jnp.concatenate(
            [first.reshape(nexp, 1, 8, rstep), second.reshape(nexp, 1, 8, rstep)], axis=1
        ).reshape(count, rstep)

    def unpack(k, r):
        merged = merge(lambda rs, cs: trecv[k, :, :, r, rs, cs])
        main = trecv[k, :, :, r, :, :].reshape(count, rwide)
        xraw[:, block(r)] = jnp.concatenate([main, merged.astype(BF16)], axis=1)
        mf = main.astype(F32)
        return sum(
            (mf[:, q * rstep : (q + 1) * rstep] * mf[:, q * rstep : (q + 1) * rstep] for q in range(3)),
            merged * merged,
        )

    def gate_up(k, squares):
        total = jnp.sum(squares[0] + squares[1] + (squares[2] + squares[3]), axis=1, keepdims=True)
        scale = lax.rsqrt(total * (1.0 / width) + 0.5)
        x = (xraw[...].astype(F32) * scale * gns[...]).astype(BF16)
        ga = lax.dot_general(wbuf[0], x, NT, preferred_element_type=F32)
        ua = lax.dot_general(wbuf[1], x, NT, preferred_element_type=F32)
        kept = lax.rem(lax.broadcasted_iota(jnp.int32, ga.shape, 1), SLOTS) < CAP
        h = jnp.where(kept, ga / (1.0 + jnp.exp(-ga)) * ua, 0.0).astype(BF16)
        hid[k, d] = h
        return h

    def hid_half(k, x, p):
        return hid.at[k, x, pl.ds(p * half, half)]

    def share_hidden(k):
        for q in range(2):
            for j, n in enumerate((1, ndp - 1)):
                part = hid_half(k, d, j if q == 0 else 1 - j)
                rs = hrs.at[k, j] if q == 0 else hns.at[k]
                rc(part, part, s_h, rs, at_x(n)).start()

    def forward_hidden(k):
        for j, n in enumerate((1, ndp - 1)):
            part = hid_half(k, lax.rem(d + ndp - n, ndp), j)
            arrived(hrs.at[k, j], part)
            rc(part, part, s_h, hfr.at[k], at_x(n)).start()

    def wait_hidden(k):
        arrived(hns.at[k], hid.at[k, 0])
        arrived(hfr.at[k], hid.at[k, 0])

    hy = ny // 2

    def share_cot():
        across = lax.rem(d + 2, ndp)
        for j, n in enumerate((1, ndp - 1)):
            src = crecv.at[pl.ds(j * hy, hy), :, across]
            rc(src, cstage.at[j], s_x, cgr.at[j], at_x(n)).start()
        for j, n in enumerate((1, ndp - 1)):
            src = crecv.at[:, :, lax.rem(d + n, ndp)]
            rc(src, cotx.at[0, d], s_x, cxr.at[j], at_x(n)).start()
        cotx[0, d] = crecv[:, :, d]
        rc(cotx.at[0, d], cotx.at[1, d], s_x, cdr, partner).start()

    def forward_cot():
        for j, n in enumerate((1, ndp - 1)):
            arrived(cgr.at[j], cstage.at[j])
            dst = cotx.at[0, lax.rem(d + ndp - n, ndp), pl.ds(j * hy, hy)]
            rc(cstage.at[j], dst, s_x, cfr, at_x(n)).start()

    def spread_cot():
        for j, n in enumerate((1, ndp - 1)):
            x = lax.rem(d + ndp - n, ndp)
            arrived(cxr.at[j], cotx.at[0, x])
            rc(cotx.at[0, x], cotx.at[1, x], s_x, cdr, partner).start()
        x = lax.rem(d + 2, ndp)
        arrived(cfr, cotx.at[0, x])
        rc(cotx.at[0, x], cotx.at[1, x], s_x, cdr, partner).start()

    hrows = count // 2

    def direct(k, r, n, dest):
        return rc(rsend.at[k, r, dest], rrecv.at[k, r, y], s_r, rrs.at[k, r], at_y(n))

    def multiply(k, r, h):
        part = lax.dot_general(h, wbuf[2, :, block(r)], TN, preferred_element_type=F32)
        dsend[k, r] = part[hrows:].astype(BF16)
        rc(dsend.at[k, r], drecv.at[k, r], s_d, drs.at[k, r], partner).start()
        psum[r] = part[:hrows]

    def pack(k, r):
        with jax.named_scope(f"dw{k}{r}"):
            arrived(drs.at[k, r], drecv.at[k, r])
        total = psum[r] + drecv[k, r].astype(F32)
        t4 = total.reshape(ny, 2, 8, cols)
        lo, hi = t4[:, 0].reshape(ny * 8, cols), t4[:, 1].reshape(ny * 8, cols)
        lo3, hi3 = lo[:, rwide:], hi[:, rwide:]
        fill = jnp.concatenate([turned(lo3), lo3, turned(hi3)], axis=1)
        low = lax.rem(lax.broadcasted_iota(jnp.int32, (ny * 8, rwide), 0), 8) < 4
        hi = jnp.where(low, hi[:, :rwide], fill)
        packed = jnp.concatenate(
            [lo[:, :rwide].reshape(ny, 1, 8, rwide), hi.reshape(ny, 1, 8, rwide)], axis=1
        )
        rsend[k, r] = packed.reshape(ny, SLOTS, rwide).astype(BF16)
        rc(rsend.at[k, r, lax.rem(y + far, ny)], mrecv.at[k, r], s_m, mrs.at[k, r], mate_dev).start()

    def straight(k, r):
        for n in near:
            if n in (far - 1, far + 1):

                @pl.when(2 * far - relay_n != n)
                def _(n=n):
                    direct(k, r, n, lax.rem(y + n, ny)).start()
            else:
                direct(k, r, n, lax.rem(y + n, ny)).start()
        rrecv[k, r, y] = rsend[k, r, y]

    def finish_far(k, r):
        with jax.named_scope(f"mw{k}{r}"):
            arrived(mrs.at[k, r], mrecv.at[k, r])
        both = rsend[k, r, mate_far].astype(F32) + mrecv[k, r].astype(F32)
        rsend[k, r, mate_far] = both.astype(BF16)
        dest = (s, mate_far * 2 + c, d)
        rc(rsend.at[k, r, mate_far], rrecv.at[k, r, y], s_r, rrs.at[k, r], dest).start()

    def zcopy(r, sec):
        cs = block(r)
        return rc(obuf.at[0, :, cs], xin.at[1, :, cs], s_z, zrs.at[r], (sec, i, d))

    def combine(k, r):
        cs = block(r)
        with jax.named_scope(f"rw{k}{r}"):
            arrived(rrs.at[k, r], rrecv.at[k, r, pl.ds(0, len(near))])
        got = rrecv[k, r].reshape(ny * SLOTS, rwide)
        folded = jnp.concatenate([got[:, q * rstep : (q + 1) * rstep] for q in range(3)], axis=0)
        res = xin[k, :, cs].astype(F32) + jnp.concatenate(
            [
                jnp.dot(mix[k], got, preferred_element_type=F32),
                jnp.dot(mixs[k], folded, preferred_element_type=F32),
            ],
            axis=1,
        )
        obuf[k, :, cs] = res.astype(BF16)
        if k == 0:

            @pl.when(s < nsec - 1)
            def _():
                zcopy(r, s + 1).start()

    def zwait(r):
        with jax.named_scope(f"zw{r}"):

            @pl.when(s > 0)
            def _():
                zcopy(r, s - 1).wait_recv()

            if r == 0:

                @pl.when(s == 0)
                def _():
                    l_fresh.wait()

    def cot_arrive(n):
        arrived(crs.at[n - 1], crecv.at[ysrc(n)])

    select(0)
    l_arr.wait()
    with jax.named_scope("disp0"):
        dispatch(0)
    select(1)
    for k in range(2):
        for r in range(ndp):
            rrecv[k, r, lax.rem(y + far, ny)] = jnp.zeros((SLOTS, rwide), BF16)
    l_cot.wait()
    for k in range(2):
        for b in range(ndp):

            def put(cs, v, k=k, b=b):
                csend[:, k, b, :, cs] = v

            pick(selgb, k, cin[k, :, b * cols : (b + 1) * cols], put)
    with jax.named_scope("rel0"):
        relay(0)
    with jax.named_scope("spr0"):
        spread(0)
    for n in near:
        dest = lax.rem(y + n, ny)
        rc(csend.at[lax.div(dest, 2)], crecv.at[y], s_c, crs.at[n - 1], at_y(n)).start()
    crecv[y] = csend[lax.div(y, 2)]
    with jax.named_scope("fw0"):
        forward_w(0)
    with jax.named_scope("fw1"):
        forward_w(1)
    send_w(2, wd)
    with jax.named_scope("wspr0"):
        wait_spread(0)
    l_gn.wait()
    squares = [unpack(0, r) for r in range(ndp)]
    with jax.named_scope("cotm"):
        blk = crecv.at[mate_far]
        arrived(crs.at[relay_n - 1], blk)
        rc(blk, blk, s_c, crs.at[far - 1], mate_dev).start()
    l_w[0].wait()
    l_w[1].wait()
    with jax.named_scope("near01"):
        wait_near(0)
        wait_near(1)
    with jax.named_scope("far01"):
        wait_far(0)
        wait_far(1)
    with jax.named_scope("gu0"):
        h = gate_up(0, squares)
    l_w[2].wait()
    multiply(0, 0, h)
    with jax.named_scope("fw2"):
        forward_w(2)
    share_hidden(0)
    pack(0, 0)
    straight(0, 0)
    with jax.named_scope("cotw"):
        for n in near:
            if n in (far - 1, far + 1):

                @pl.when(relay_n != n)
                def _(n=n):
                    cot_arrive(n)
            else:
                cot_arrive(n)
        cot_arrive(far)
    share_cot()
    finish_far(0, 0)
    with jax.named_scope("near2"):
        wait_near(2)
    for r in (1, 2):
        multiply(0, r, h)
    for r in (1, 2):
        pack(0, r)
        straight(0, r)
    combine(0, 0)
    with jax.named_scope("far2"):
        wait_far(2)
    multiply(0, 3, h)
    pack(0, 3)
    straight(0, 3)
    for r in (1, 2, 3):
        finish_far(0, r)
    combine(0, 1)
    combine(0, 2)

    zwait(0)
    dispatch(1)
    combine(0, 3)
    out0 = pltpu.make_async_copy(obuf.at[0], out.at[0], lsem.at[6])
    out0.start()
    with jax.named_scope("fh0"):
        forward_hidden(0)
    for r in (1, 2):
        zwait(r)
        dispatch(r + 1)
    with jax.named_scope("rel1"):
        relay(1)
    with jax.named_scope("fc"):
        forward_cot()
    zwait(3)
    dispatch(4)
    with jax.named_scope("rel23"):
        relay(2)
        relay(3)
    with jax.named_scope("spr12"):
        spread(1)
        spread(2)
    with jax.named_scope("rel4"):
        relay(4)
    with jax.named_scope("spr3"):
        spread(3)
    squares = []
    for r in range(3):
        wait_spread(r + 1)
        squares.append(unpack(1, r))
    with jax.named_scope("spr4"):
        spread(4)
    with jax.named_scope("wspr4"):
        wait_spread(4)
    squares.append(unpack(1, 3))
    with jax.named_scope("gu1"):
        h = gate_up(1, squares)
    share_hidden(1)
    for r in range(ndp):
        multiply(1, r, h)
    for r in range(ndp):
        pack(1, r)
    for r in range(ndp):
        straight(1, r)
    finish_far(1, 0)
    with jax.named_scope("fh1"):
        forward_hidden(1)
    for r in range(1, ndp):
        finish_far(1, r)

    with jax.named_scope("sc"):
        spread_cot()
    with jax.named_scope("wsc"):
        arrived(cdr, cotx.at[1])
    for k in range(2):
        with jax.named_scope(f"wh{k}"):
            wait_hidden(k)
        with jax.named_scope(f"grad{k}"):
            for x in range(ndp):
                merged = merge(lambda rs, cs, x=x, k=k: cotx[:, x, :, k, rs, cs]).astype(BF16)
                main = cotx[:, x, :, k].reshape(count, rwide)
                cr = jnp.concatenate([main, merged], axis=1)
                add = jnp.dot(hid[k, x], cr, preferred_element_type=F32)
                if k == 0 and x == 0:
                    gacc[...] = add
                else:
                    gacc[...] += add
    gout = pltpu.make_async_copy(gacc, grad_out, lsem.at[7])
    gout.start()
    for r in range(ndp):
        combine(1, r)
    out1 = pltpu.make_async_copy(obuf.at[1], out.at[1], lsem.at[8])
    out1.start()
    with jax.named_scope("tail"):
        drain(s_w, wbuf.at[:, :, pl.ds(0, 3 * cols)])
        drain(s_t, trecv.at[0])
        drain(s_t, trecv.at[1, :, pl.ds(0, ny - 1)])
        drain(s_c, crecv.at[pl.ds(0, ny - 1)])
        drain(s_x, cotx.at[1])
        drain(s_x, cotx.at[0, pl.ds(0, 3)])
        drain(s_x, cstage)
        drain(s_h, hid.at[:, pl.ds(0, 3)])
        drain(s_d, drecv)
        drain(s_m, mrecv)
        drain(s_r, rrecv.at[:, :, pl.ds(0, len(near))])
    with jax.named_scope("zs"):

        @pl.when(s < nsec - 1)
        def _():
            drain(s_z, obuf.at[0])

    with jax.named_scope("outw"):
        out0.wait()
        gout.wait()
        out1.wait()


def local(nsec, nexp, ndp, arrivals, fresh, routes, gates, cotangent, norm_gain, w_gate, w_up, w_down):
    tok, width = arrivals.shape[1:]
    hidn, cols = w_gate.shape[1:]
    flight = nexp // SPLIT
    ny = nexp // 2
    steps = routes.shape[1]
    rows = nexp * SLOTS
    routes_t = jnp.transpose(routes[0], (2, 0, 1))
    gates_t = jnp.transpose(gates[0], (2, 0, 1))
    rwide = cols // 4 * 3
    any_spec = pl.BlockSpec(memory_space=pl.ANY)
    hbm_spec = pl.BlockSpec(memory_space=pltpu.HBM)
    dma = pltpu.SemaphoreType.DMA
    out, grad = pl.pallas_call(
        functools.partial(kernel_body, nsec, nexp, ndp),
        name="moe_relay",
        out_shape=(
            jax.ShapeDtypeStruct((steps, tok, width), BF16),
            jax.ShapeDtypeStruct((hidn, cols), F32),
        ),
        in_specs=[hbm_spec] * 9,
        out_specs=(any_spec, any_spec),
        scratch_shapes=[
            pltpu.VMEM((2, tok, width), BF16),
            pltpu.VMEM((2, tok, width), BF16),
            pltpu.VMEM((3, hidn, width), BF16),
            pltpu.VMEM((2, flight, ndp, SLOTS, rwide), BF16),
            pltpu.VMEM((2, 2, ny, ndp, SLOTS, rwide), BF16),
            pltpu.VMEM((rows, width), BF16),
            pltpu.VMEM((flight, 2, ndp, SLOTS, rwide), BF16),
            pltpu.VMEM((ny, 2, ndp, SLOTS, rwide), BF16),
            pltpu.VMEM((2, ny // 2, 2, SLOTS, rwide), BF16),
            pltpu.VMEM((2, ndp, ny, 2, SLOTS, rwide), BF16),
            pltpu.VMEM((2, ndp, hidn, rows), BF16),
            pltpu.VMEM((2, ndp, rows // 2, cols), BF16),
            pltpu.VMEM((2, ndp, rows // 2, cols), BF16),
            pltpu.VMEM((ndp, rows // 2, cols), F32),
            pltpu.VMEM((2, ndp, ny, SLOTS, rwide), BF16),
            pltpu.VMEM((2, ndp, SLOTS, rwide), BF16),
            pltpu.VMEM((2, ndp, ny, SLOTS, rwide), BF16),
            pltpu.VMEM(routes_t.shape, jnp.int32),
            pltpu.VMEM(gates_t.shape, BF16),
            pltpu.VMEM((1, width), F32),
            pltpu.VMEM((2, 3, flight * SLOTS, 2 * tok), BF16),
            pltpu.VMEM((2, 3, flight * SLOTS, 2 * tok), BF16),
            pltpu.VMEM((2, tok, ny * SLOTS), BF16),
            pltpu.VMEM((2, tok, 3 * ny * SLOTS), BF16),
            pltpu.VMEM((2, tok, width), BF16),
            pltpu.VMEM((hidn, cols), F32),
            dma((12,)), dma((9,)),
            dma((3, 2)), dma((3,)), dma((3,)),
            dma((1 + ndp, ny - 1)), dma((1 + ndp,)),
            dma((ny - 1,)), dma((2,)), dma((2,)), dma(()), dma(()),
            dma((2, 2)), dma((2,)), dma((2,)),
            dma((2, ndp)), dma((2, ndp)), dma((2, ndp)), dma((ndp,)),
        ],
        compiler_params=pltpu.CompilerParams(
            collective_id=0, has_side_effects=True, vmem_limit_bytes=24 * 1024 * 1024
        ),
    )(
        *(
            pltpu.with_memory_space_constraint(a, pltpu.HBM)
            for a in (
                arrivals[0], fresh[0], routes_t, gates_t, cotangent[0], norm_gain, w_gate[0], w_up[0], w_down[0]
            )
        )
    )
    return out[None], grad[None]


def solution(mesh):
    placed = (
        P("section", ("expert", "dp"), None),
        P(None, ("expert", "dp"), None),
        P("section", None, ("expert", "dp"), None),
        P("section", None, ("expert", "dp"), None),
        P("section", None, ("expert", "dp"), None),
        P("section", None),
        P("section", "expert", "dp"),
        P("section", "expert", "dp"),
        P("section", "expert", "dp"),
    )
    return jax.shard_map(
        functools.partial(local, mesh.shape["section"], mesh.shape["expert"], mesh.shape["dp"]),
        mesh=mesh,
        in_specs=placed,
        out_specs=(P("section", None, ("expert", "dp"), None), P("section", "expert", "dp")),
        check_vma=False,
    )
```

time: 106 us -> 81.9 us (0.77)
  the two profiles are of different devices: /device:TPU:256 before, /device:TPU:1 now
where the time goes in v3:
time: 81.9 us; the launch traced here: 81.4 us
  Pallas kernels  79.1 us (97%)
  local copies, waits for them, and re-layouts  1.65 us (2%)
    pallas_call x1, Pallas kernels, local(): pl.pallas_call(functools.partial(kernel_body, nsec, nexp, ndp), name='moe...  79.1 us
    unnamed x2, local copies, waits for them, and re-layouts  1.65 us

profile of v3, /device:TPU:1, one launch (start us, length us, event | category | flops | bytes accessed | tf_op | source)
XLA Modules:
  0.0 81.4 jit_solution(13796063096849693711)
XLA Ops:
  0.6 79.1 %moe_relay.1 = (bf16[2,64,2048]{2,1,0:T(8,128)(2,1)S(1)}, f32[352,512]{1,0:T(8,128)S(1)}) custom-call(bf16[64,2048]{1,0:T(8,128)(2,1)} %bitcast.20, bf16[64,2048]{1,0:T(8,128)(2,1)} %bitcast.21, s32[6,2,64]{2,1,0:T(2,128)} %bitcast.22, bf16[6,2,64]{2,1,0:T(2,128)(2,1)} %bitcast.23, bf16[2,64,2048]{2,1,0:T(8,128)(2,1)} %bitcast.16, f32[1,2048]{1,0:T(1,128)} %gain.1, ...), custom_call_target="tpu_custom_call" | custom-call | tf_op jit(solution)/shard_map/moe_relay/pallas_call | solution.py:609
  79.8 0.8 copy.13
  80.6 0.9 %copy.14 = f32[1,352,512]{2,1,0:T(8,128)} copy(f32[1,352,512]{2,1,0:T(8,128)S(1)} %bitcast.14) | data formatting | bytes 1441792

commit v4 on v3

--- a/solution.py
+++ b/solution.py
@@ -14,7 +14,6 @@
 ORDER = (0, 1, 3, 2)
 MESH = pl.DeviceIdType.MESH
 NT = (((1,), (1,)), ((), ()))
-TN = (((0,), (0,)), ((), ()))
 F32 = jnp.float32
 BF16 = jnp.bfloat16
 
@@ -23,7 +22,7 @@
     nsec, nexp, ndp,
     arr, fresh, routes, gates, cot, gain, wg, wu, wd,
     out, grad_out,
-    xin, cin, wbuf, tsend, trecv, xraw, csend, crecv, cstage, cotx, hid, dsend, drecv, psum, rsend, mrecv, rrecv,
+    xin, cin, wbuf, tsend, trecv, xraw, acts, csend, crecv, cstage, cotx, hid, dsend, drecv, psum, rsend, mrecv, rrecv,
     rts, gts, gns, selb, selgb, mix, mixs, obuf, gacc,
     lsem, sends, wrs, wns, frs, trs, tdr, crs, cxr, cgr, cfr, cdr, hrs, hns, hfr, drs, mrs, rrs, zrs,
 ):
@@ -85,12 +84,12 @@
     l_rt = pltpu.make_async_copy(routes, rts, lsem.at[9])
     l_gt = pltpu.make_async_copy(gates, gts, lsem.at[10])
     l_gn = pltpu.make_async_copy(gain, gns, lsem.at[11])
-    l_gn.start()
+    for l in l_w:
+        l.start()
     l_rt.start()
     l_gt.start()
     l_arr.start()
-    for l in l_w:
-        l.start()
+    l_gn.start()
     l_cot.start()
 
     @pl.when(s == 0)
@@ -98,7 +97,7 @@
         l_fresh.start()
 
     bar = pltpu.get_barrier_semaphore()
-    peers = [at_x(k) for k in range(1, ndp)] + [at_y(n) for n in near] + [partner]
+    peers = [at_x(k) for k in range(1, ndp)] + [at_y(n) for n in range(1, ny)] + [partner]
     for p in peers:
         pl.semaphore_signal(bar, inc=1, device_id=p, device_id_type=MESH)
 
@@ -117,14 +116,16 @@
         )
 
     def part_of(w, j, own):
-        return w.at[pl.ds(j * half, half), colsl(own)] if own is not None else w.at[pl.ds(j * half, half)]
-
-    def send_w(m, w):
+        return w.at[pl.ds(j * half, half), colsl(own)]
+
+    def send_w(m):
+        l_w[m].wait()
         for q in range(2):
             for j, k in enumerate((1, ndp - 1)):
                 p = j if q == 0 else 1 - j
                 rs = wrs.at[m, j] if q == 0 else wns.at[m]
-                rc(part_of(w, p, None), part_of(wbuf.at[m], p, d), s_w, rs, at_x(k)).start()
+                part = part_of(wbuf.at[m], p, d)
+                rc(part, part, s_w, rs, at_x(k)).start()
 
     def forward_w(m):
         for j, k in enumerate((1, ndp - 1)):
@@ -138,8 +139,8 @@
     def wait_far(m):
         arrived(frs.at[m], wbuf.at[m, :, pl.ds(0, cols)])
 
-    send_w(0, wg)
-    send_w(1, wu)
+    send_w(0)
+    send_w(1)
 
     pos = lax.rem(lax.broadcasted_iota(jnp.int32, (rows, tok), 0), SLOTS)
     tail = SLOTS - CAP
@@ -204,7 +205,7 @@
                 tsend[k, :, r, :, cs] = v
 
             pick(selb, k, xin[k, :, block(r)], put)
-        for n in near:
+        for n in [far] * (m == ndp) + near:
             dest = lax.rem(y + n, ny)
             src = view(tsend, m, lax.div(dest, 2))
             rc(src, view(trecv, m, 0, y), s_t, trs.at[m, n - 1], at_y(n)).start()
@@ -227,13 +228,14 @@
 
     def spread(m):
         for n in near[::-1]:
-            if n in (far - 1, far + 1):
+            if n in (far - 1, far + 1) and m < ndp:
 
                 @pl.when(relay_n != n)
                 def _(n=n):
                     onward(m, ysrc(n), n)
             else:
                 onward(m, ysrc(n), n)
+    def spread_far(m):
         onward(m, ysrc(far), far)
 
     def wait_spread(m):
@@ -259,24 +261,35 @@
 
     def unpack(k, r):
         merged = merge(lambda rs, cs: trecv[k, :, :, r, rs, cs])
-        main = trecv[k, :, :, r, :, :].reshape(count, rwide)
-        xraw[:, block(r)] = jnp.concatenate([main, merged.astype(BF16)], axis=1)
-        mf = main.astype(F32)
+        mf = trecv[k, :, :, r, :, :].reshape(count, rwide).astype(F32)
+        whole = jnp.concatenate([mf, merged], axis=1)
+        xraw[r] = (whole * gns[:, block(r)]).astype(BF16)
         return sum(
             (mf[:, q * rstep : (q + 1) * rstep] * mf[:, q * rstep : (q + 1) * rstep] for q in range(3)),
             merged * merged,
         )
 
+    def project(r):
+        for m in range(2):
+            part = lax.dot_general(wbuf[m, :, block(r)], xraw[r], NT, preferred_element_type=F32)
+            if r == 0:
+                acts[m] = part
+            else:
+                acts[m] += part
+
     def gate_up(k, squares):
-        total = jnp.sum(squares[0] + squares[1] + (squares[2] + squares[3]), axis=1, keepdims=True)
-        scale = lax.rsqrt(total * (1.0 / width) + 0.5)
-        x = (xraw[...].astype(F32) * scale * gns[...]).astype(BF16)
-        ga = lax.dot_general(wbuf[0], x, NT, preferred_element_type=F32)
-        ua = lax.dot_general(wbuf[1], x, NT, preferred_element_type=F32)
+        total = squares[0] + squares[1] + (squares[2] + squares[3])
+        high = total.astype(BF16)
+        parts = jnp.concatenate([high, (total - high.astype(F32)).astype(BF16)], axis=1)
+        ones = jnp.ones((8, 2 * rstep), BF16)
+        sums = lax.dot_general(ones, parts, NT, preferred_element_type=F32)[:1]
+        scale = lax.rsqrt(sums * (1.0 / width) + 0.5)
+        ga = acts[0] * scale
+        ua = acts[1] * scale
         kept = lax.rem(lax.broadcasted_iota(jnp.int32, ga.shape, 1), SLOTS) < CAP
-        h = jnp.where(kept, ga / (1.0 + jnp.exp(-ga)) * ua, 0.0).astype(BF16)
-        hid[k, d] = h
-        return h
+        h = jnp.where(kept, ga / (1.0 + jnp.exp(-ga)) * ua, 0.0)
+        hid[k, d] = h.astype(BF16)
+        return jnp.transpose(h).astype(BF16)
 
     def hid_half(k, x, p):
         return hid.at[k, x, pl.ds(p * half, half)]
@@ -331,8 +344,11 @@
     def direct(k, r, n, dest):
         return rc(rsend.at[k, r, dest], rrecv.at[k, r, y], s_r, rrs.at[k, r], at_y(n))
 
+    def urgent(k, r):
+        return k == 0 and r == ndp - 1
+
     def multiply(k, r, h):
-        part = lax.dot_general(h, wbuf[2, :, block(r)], TN, preferred_element_type=F32)
+        part = jnp.dot(h, wbuf[2, :, block(r)], preferred_element_type=F32)
         dsend[k, r] = part[hrows:].astype(BF16)
         rc(dsend.at[k, r], drecv.at[k, r], s_d, drs.at[k, r], partner).start()
         psum[r] = part[:hrows]
@@ -351,11 +367,12 @@
             [lo[:, :rwide].reshape(ny, 1, 8, rwide), hi.reshape(ny, 1, 8, rwide)], axis=1
         )
         rsend[k, r] = packed.reshape(ny, SLOTS, rwide).astype(BF16)
-        rc(rsend.at[k, r, lax.rem(y + far, ny)], mrecv.at[k, r], s_m, mrs.at[k, r], mate_dev).start()
+        if not urgent(k, r):
+            rc(rsend.at[k, r, lax.rem(y + far, ny)], mrecv.at[k, r], s_m, mrs.at[k, r], mate_dev).start()
 
     def straight(k, r):
-        for n in near:
-            if n in (far - 1, far + 1):
+        for n in [far] * urgent(k, r) + near:
+            if n in (far - 1, far + 1) and not urgent(k, r):
 
                 @pl.when(2 * far - relay_n != n)
                 def _(n=n):
@@ -379,7 +396,7 @@
     def combine(k, r):
         cs = block(r)
         with jax.named_scope(f"rw{k}{r}"):
-            arrived(rrs.at[k, r], rrecv.at[k, r, pl.ds(0, len(near))])
+            arrived(rrs.at[k, r], rrecv.at[k, r, pl.ds(0, len(near) + urgent(k, r))])
         got = rrecv[k, r].reshape(ny * SLOTS, rwide)
         folded = jnp.concatenate([got[:, q * rstep : (q + 1) * rstep] for q in range(3)], axis=0)
         res = xin[k, :, cs].astype(F32) + jnp.concatenate(
@@ -390,6 +407,7 @@
             axis=1,
         )
         obuf[k, :, cs] = res.astype(BF16)
+        pltpu.make_async_copy(obuf.at[k, :, cs], out.at[k, :, cs], lsem.at[6 + k]).start()
         if k == 0:
 
             @pl.when(s < nsec - 1)
@@ -419,7 +437,8 @@
     select(1)
     for k in range(2):
         for r in range(ndp):
-            rrecv[k, r, lax.rem(y + far, ny)] = jnp.zeros((SLOTS, rwide), BF16)
+            if not urgent(k, r):
+                rrecv[k, r, lax.rem(y + far, ny)] = jnp.zeros((SLOTS, rwide), BF16)
     l_cot.wait()
     for k in range(2):
         for b in range(ndp):
@@ -432,6 +451,7 @@
         relay(0)
     with jax.named_scope("spr0"):
         spread(0)
+        spread_far(0)
     for n in near:
         dest = lax.rem(y + n, ny)
         rc(csend.at[lax.div(dest, 2)], crecv.at[y], s_c, crs.at[n - 1], at_y(n)).start()
@@ -440,7 +460,7 @@
         forward_w(0)
     with jax.named_scope("fw1"):
         forward_w(1)
-    send_w(2, wd)
+    send_w(2)
     with jax.named_scope("wspr0"):
         wait_spread(0)
     l_gn.wait()
@@ -449,17 +469,17 @@
         blk = crecv.at[mate_far]
         arrived(crs.at[relay_n - 1], blk)
         rc(blk, blk, s_c, crs.at[far - 1], mate_dev).start()
-    l_w[0].wait()
-    l_w[1].wait()
     with jax.named_scope("near01"):
         wait_near(0)
         wait_near(1)
+    for r in range(ndp - 1):
+        project(r)
     with jax.named_scope("far01"):
         wait_far(0)
         wait_far(1)
+    project(ndp - 1)
     with jax.named_scope("gu0"):
         h = gate_up(0, squares)
-    l_w[2].wait()
     multiply(0, 0, h)
     with jax.named_scope("fw2"):
         forward_w(2)
@@ -484,23 +504,22 @@
         multiply(0, r, h)
     for r in (1, 2):
         pack(0, r)
+    for r in (1, 2):
         straight(0, r)
     combine(0, 0)
+    finish_far(0, 1)
+    finish_far(0, 2)
     with jax.named_scope("far2"):
         wait_far(2)
     multiply(0, 3, h)
     pack(0, 3)
     straight(0, 3)
-    for r in (1, 2, 3):
-        finish_far(0, r)
     combine(0, 1)
     combine(0, 2)
 
     zwait(0)
     dispatch(1)
     combine(0, 3)
-    out0 = pltpu.make_async_copy(obuf.at[0], out.at[0], lsem.at[6])
-    out0.start()
     with jax.named_scope("fh0"):
         forward_hidden(0)
     for r in (1, 2):
@@ -515,30 +534,42 @@
     with jax.named_scope("rel23"):
         relay(2)
         relay(3)
-    with jax.named_scope("spr12"):
+    with jax.named_scope("spr123"):
         spread(1)
         spread(2)
-    with jax.named_scope("rel4"):
-        relay(4)
-    with jax.named_scope("spr3"):
         spread(3)
+        spread_far(1)
+        spread_far(2)
     squares = []
-    for r in range(3):
+    for r in range(2):
         wait_spread(r + 1)
         squares.append(unpack(1, r))
+        project(r)
     with jax.named_scope("spr4"):
         spread(4)
+        spread_far(4)
+    with jax.named_scope("spr3"):
+        spread_far(3)
+    with jax.named_scope("wspr3"):
+        wait_spread(3)
+    squares.append(unpack(1, 2))
+    project(2)
     with jax.named_scope("wspr4"):
         wait_spread(4)
     squares.append(unpack(1, 3))
+    project(3)
     with jax.named_scope("gu1"):
         h = gate_up(1, squares)
     share_hidden(1)
-    for r in range(ndp):
-        multiply(1, r, h)
-    for r in range(ndp):
+    multiply(1, 0, h)
+    multiply(1, 1, h)
+    pack(1, 0)
+    straight(1, 0)
+    multiply(1, 2, h)
+    multiply(1, 3, h)
+    for r in range(1, ndp):
         pack(1, r)
-    for r in range(ndp):
+    for r in range(1, ndp):
         straight(1, r)
     finish_far(1, 0)
     with jax.named_scope("fh1"):
@@ -563,12 +594,10 @@
                     gacc[...] = add
                 else:
                     gacc[...] += add
-    gout = pltpu.make_async_copy(gacc, grad_out, lsem.at[7])
+    gout = pltpu.make_async_copy(gacc, grad_out, lsem.at[8])
     gout.start()
     for r in range(ndp):
         combine(1, r)
-    out1 = pltpu.make_async_copy(obuf.at[1], out.at[1], lsem.at[8])
-    out1.start()
     with jax.named_scope("tail"):
         drain(s_w, wbuf.at[:, :, pl.ds(0, 3 * cols)])
         drain(s_t, trecv.at[0])
@@ -579,8 +608,10 @@
         drain(s_x, cstage)
         drain(s_h, hid.at[:, pl.ds(0, 3)])
         drain(s_d, drecv)
-        drain(s_m, mrecv)
+        drain(s_m, mrecv.at[0, pl.ds(0, ndp - 1)])
+        drain(s_m, mrecv.at[1])
         drain(s_r, rrecv.at[:, :, pl.ds(0, len(near))])
+        drain(s_r, rrecv.at[0, 0, 0])
     with jax.named_scope("zs"):
 
         @pl.when(s < nsec - 1)
@@ -588,9 +619,18 @@
             drain(s_z, obuf.at[0])
 
     with jax.named_scope("outw"):
-        out0.wait()
         gout.wait()
-        out1.wait()
+        for k in range(2):
+            pltpu.make_async_copy(obuf.at[k], out.at[k], lsem.at[6 + k]).wait()
+
+
+def store_body(out, grad, out_hbm, grad_hbm, sem):
+    a = pltpu.make_async_copy(out, out_hbm, sem.at[0])
+    b = pltpu.make_async_copy(grad, grad_hbm, sem.at[1])
+    a.start()
+    b.start()
+    a.wait()
+    b.wait()
 
 
 def local(nsec, nexp, ndp, arrivals, fresh, routes, gates, cotangent, norm_gain, w_gate, w_up, w_down):
@@ -621,7 +661,8 @@
             pltpu.VMEM((3, hidn, width), BF16),
             pltpu.VMEM((2, flight, ndp, SLOTS, rwide), BF16),
             pltpu.VMEM((2, 2, ny, ndp, SLOTS, rwide), BF16),
-            pltpu.VMEM((rows, width), BF16),
+            pltpu.VMEM((ndp, rows, cols), BF16),
+            pltpu.VMEM((2, hidn, rows), F32),
             pltpu.VMEM((flight, 2, ndp, SLOTS, rwide), BF16),
             pltpu.VMEM((ny, 2, ndp, SLOTS, rwide), BF16),
             pltpu.VMEM((2, ny // 2, 2, SLOTS, rwide), BF16),
@@ -660,6 +701,15 @@
             )
         )
     )
+    out, grad = pl.pallas_call(
+        store_body,
+        name="store",
+        out_shape=(jax.ShapeDtypeStruct(out.shape, BF16), jax.ShapeDtypeStruct(grad.shape, F32)),
+        in_specs=(any_spec, any_spec),
+        out_specs=(any_spec, any_spec),
+        scratch_shapes=[dma((2,))],
+        compiler_params=pltpu.CompilerParams(vmem_limit_bytes=1024 * 1024),
+    )(out, grad)
     return out[None], grad[None]
 
 

time: 81.9 us -> 79.7 us (0.973)
  local copies, waits for them, and re-layouts: 1.65 us -> 0 us
  Pallas kernels: 79.1 us -> 77.9 us
    pallas_call x1, Pallas kernels: 79.1 us -> 76.8 us  [local(): pl.pallas_call(functools.partial(kernel_body, nsec, nexp, ndp), name='moe...]
    unnamed x2 -> x0, local copies, waits for them, and re-layouts: 1.65 us -> none
    pallas_call x0 -> x1, Pallas kernels: none -> 1.05 us  [local(): pl.pallas_call(store_body, name='store', out_shape=(jax.ShapeDtypeStruct(...]
where the time goes in v4:
time: 79.7 us; the launch traced here: 78.5 us
  Pallas kernels  77.9 us (98%)
    pallas_call x1, Pallas kernels, local(): pl.pallas_call(functools.partial(kernel_body, nsec, nexp, ndp), name='moe...  76.8 us

profile of v4, /device:TPU:1, one launch (start us, length us, event | category | flops | bytes accessed | tf_op | source)
XLA Modules:
  0.0 78.5 jit_solution(8817832652291665674)
XLA Ops:
  0.6 76.8 %moe_relay.1 = (bf16[2,64,2048]{2,1,0:T(8,128)(2,1)S(1)}, f32[352,512]{1,0:T(8,128)S(1)}) custom-call(bf16[64,2048]{1,0:T(8,128)(2,1)} %bitcast.18, bf16[64,2048]{1,0:T(8,128)(2,1)} %bitcast.19, s32[6,2,64]{2,1,0:T(2,128)} %bitcast.20, bf16[6,2,64]{2,1,0:T(2,128)(2,1)} %bitcast.21, bf16[2,64,2048]{2,1,0:T(8,128)(2,1)} %bitcast.14, f32[1,2048]{1,0:T(1,128)} %gain.1, ...), custom_call_target="tpu_custom_call" | custom-call | tf_op jit(solution)/shard_map/moe_relay/pallas_call | solution.py:649
  77.4 1.1 %store.1 = (bf16[2,64,2048]{2,1,0:T(8,128)(2,1)}, f32[352,512]{1,0:T(8,128)}) custom-call(bf16[2,64,2048]{2,1,0:T(8,128)(2,1)S(1)} %get-tuple-element.6.out, f32[352,512]{1,0:T(8,128)S(1)} %get-tuple-element.7.grad), custom_call_target="tpu_custom_call" | custom-call | tf_op jit(solution)/shard_map/store/pallas_call | solution.py:704

commit v5 on v4

--- a/solution.py
+++ b/solution.py
@@ -10,8 +10,8 @@
 SPLIT = 4
 CAP = 12
 SLOTS = 16
+DIRECT = 3
 NEAR = (3, 5, 2, 6, 1, 7)
-ORDER = (0, 1, 3, 2)
 MESH = pl.DeviceIdType.MESH
 NT = (((1,), (1,)), ((), ()))
 F32 = jnp.float32
@@ -35,6 +35,7 @@
     tok, width = arr.shape
     hidn, cols = wg.shape
     half = hidn // 2
+    hc = cols // 2
     rwide = rsend.shape[4]
     rstep = rwide // 3
     far = ny // 2
@@ -74,13 +75,44 @@
     def arrived(sem, ref):
         rc(ref, ref, sem, sem, partner).wait_recv()
 
-    l_arr = pltpu.make_async_copy(arr, xin.at[0], lsem.at[0])
+    near_dp, far_dp = (lax.rem(d + ndp - 1, ndp), lax.rem(d + 1, ndp)), lax.rem(d + 2, ndp)
+    HALVES = (
+        ((d, 0), (d, 1)),
+        ((near_dp[0], 0), (near_dp[1], 1)),
+        ((near_dp[0], 1), (near_dp[1], 0)),
+        ((far_dp, 0), (far_dp, 1)),
+    )
+
+    def hs(owner, j):
+        return pl.ds(pl.multiple_of(owner * cols + j * hc, hc), hc)
+
+    def pieces(r):
+        return [(hs(o, j), slice(q * hc, (q + 1) * hc)) for q, (o, j) in enumerate(HALVES[r])]
+
+    def by_block(src, dst, sem, back=False):
+        for r in range(ndp):
+            for natural, local in pieces(r):
+                a, b = src.at[:, natural], dst.at[r, :, local]
+                pltpu.make_async_copy(a, b, sem).start()
+
+    bar = pltpu.get_barrier_semaphore()
+    peers = [at_x(k) for k in range(1, ndp)] + [at_y(n) for n in range(1, ny)] + [partner]
+    for p in peers:
+        pl.semaphore_signal(bar, inc=1, device_id=p, device_id_type=MESH)
+
+    @pl.when(s > 0)
+    def _():
+        pl.semaphore_signal(bar, inc=1, device_id=(s - 1, i, d), device_id_type=MESH)
+
+    @pl.when(s < nsec - 1)
+    def _():
+        pl.semaphore_signal(bar, inc=1, device_id=(s + 1, i, d), device_id_type=MESH)
+
     l_cot = pltpu.make_async_copy(cot, cin, lsem.at[1])
     l_w = [
         pltpu.make_async_copy(w, wbuf.at[m, :, colsl(d)], lsem.at[2 + m])
         for m, w in enumerate((wg, wu, wd))
     ]
-    l_fresh = pltpu.make_async_copy(fresh, xin.at[1], lsem.at[5])
     l_rt = pltpu.make_async_copy(routes, rts, lsem.at[9])
     l_gt = pltpu.make_async_copy(gates, gts, lsem.at[10])
     l_gn = pltpu.make_async_copy(gain, gns, lsem.at[11])
@@ -88,26 +120,13 @@
         l.start()
     l_rt.start()
     l_gt.start()
-    l_arr.start()
+    by_block(arr, xin.at[0], lsem.at[0])
     l_gn.start()
     l_cot.start()
 
     @pl.when(s == 0)
     def _():
-        l_fresh.start()
-
-    bar = pltpu.get_barrier_semaphore()
-    peers = [at_x(k) for k in range(1, ndp)] + [at_y(n) for n in range(1, ny)] + [partner]
-    for p in peers:
-        pl.semaphore_signal(bar, inc=1, device_id=p, device_id_type=MESH)
-
-    @pl.when(s > 0)
-    def _():
-        pl.semaphore_signal(bar, inc=1, device_id=(s - 1, i, d), device_id_type=MESH)
-
-    @pl.when(s < nsec - 1)
-    def _():
-        pl.semaphore_signal(bar, inc=1, device_id=(s + 1, i, d), device_id_type=MESH)
+        by_block(fresh, xin.at[1], lsem.at[5])
 
     with jax.named_scope("bar"):
         pl.semaphore_wait(
@@ -115,8 +134,8 @@
             len(peers) + jnp.where(s > 0, 1, 0) + jnp.where(s < nsec - 1, 1, 0),
         )
 
-    def part_of(w, j, own):
-        return w.at[pl.ds(j * half, half), colsl(own)]
+    def part_of(m, j, owner):
+        return wbuf.at[m, :, hs(owner, j)]
 
     def send_w(m):
         l_w[m].wait()
@@ -124,12 +143,12 @@
             for j, k in enumerate((1, ndp - 1)):
                 p = j if q == 0 else 1 - j
                 rs = wrs.at[m, j] if q == 0 else wns.at[m]
-                part = part_of(wbuf.at[m], p, d)
+                part = part_of(m, p, d)
                 rc(part, part, s_w, rs, at_x(k)).start()
 
     def forward_w(m):
         for j, k in enumerate((1, ndp - 1)):
-            part = part_of(wbuf.at[m], j, lax.rem(d + ndp - k, ndp))
+            part = part_of(m, j, lax.rem(d + ndp - k, ndp))
             arrived(wrs.at[m, j], part)
             rc(part, part, s_w, frs.at[m], at_x(k)).start()
 
@@ -187,8 +206,8 @@
     def view(ref, m, *at):
         return ref.at[(0,) + at] if m == 0 else ref.at[(1,) + at + (m - 1,)]
 
-    def block(r):
-        return colsl(lax.rem(d + ORDER[r], ndp))
+    def columns(ref, r, *at):
+        return jnp.concatenate([ref[at + (natural,)] for natural, _ in pieces(r)], axis=-1)
 
     def pick(sel, k, x, put):
         last = x[:, rwide:]
@@ -204,8 +223,8 @@
             def put(cs, v, r=r):
                 tsend[k, :, r, :, cs] = v
 
-            pick(selb, k, xin[k, :, block(r)], put)
-        for n in [far] * (m == ndp) + near:
+            pick(selb, k, xin[k, r], put)
+        for n in [far] * (m >= DIRECT) + near:
             dest = lax.rem(y + n, ny)
             src = view(tsend, m, lax.div(dest, 2))
             rc(src, view(trecv, m, 0, y), s_t, trs.at[m, n - 1], at_y(n)).start()
@@ -228,7 +247,7 @@
 
     def spread(m):
         for n in near[::-1]:
-            if n in (far - 1, far + 1) and m < ndp:
+            if n in (far - 1, far + 1) and m < DIRECT:
 
                 @pl.when(relay_n != n)
                 def _(n=n):
@@ -263,7 +282,7 @@
         merged = merge(lambda rs, cs: trecv[k, :, :, r, rs, cs])
         mf = trecv[k, :, :, r, :, :].reshape(count, rwide).astype(F32)
         whole = jnp.concatenate([mf, merged], axis=1)
-        xraw[r] = (whole * gns[:, block(r)]).astype(BF16)
+        xraw[r] = (whole * columns(gns, r, slice(None))).astype(BF16)
         return sum(
             (mf[:, q * rstep : (q + 1) * rstep] * mf[:, q * rstep : (q + 1) * rstep] for q in range(3)),
             merged * merged,
@@ -271,7 +290,7 @@
 
     def project(r):
         for m in range(2):
-            part = lax.dot_general(wbuf[m, :, block(r)], xraw[r], NT, preferred_element_type=F32)
+            part = lax.dot_general(columns(wbuf, r, m, slice(None)), xraw[r], NT, preferred_element_type=F32)
             if r == 0:
                 acts[m] = part
             else:
@@ -345,10 +364,10 @@
         return rc(rsend.at[k, r, dest], rrecv.at[k, r, y], s_r, rrs.at[k, r], at_y(n))
 
     def urgent(k, r):
-        return k == 0 and r == ndp - 1
+        return k == 0
 
     def multiply(k, r, h):
-        part = jnp.dot(h, wbuf[2, :, block(r)], preferred_element_type=F32)
+        part = jnp.dot(h, columns(wbuf, r, 2, slice(None)), preferred_element_type=F32)
         dsend[k, r] = part[hrows:].astype(BF16)
         rc(dsend.at[k, r], drecv.at[k, r], s_d, drs.at[k, r], partner).start()
         psum[r] = part[:hrows]
@@ -368,7 +387,7 @@
         )
         rsend[k, r] = packed.reshape(ny, SLOTS, rwide).astype(BF16)
         if not urgent(k, r):
-            rc(rsend.at[k, r, lax.rem(y + far, ny)], mrecv.at[k, r], s_m, mrs.at[k, r], mate_dev).start()
+            rc(rsend.at[k, r, lax.rem(y + far, ny)], mrecv.at[r], s_m, mrs.at[r], mate_dev).start()
 
     def straight(k, r):
         for n in [far] * urgent(k, r) + near:
@@ -383,31 +402,30 @@
 
     def finish_far(k, r):
         with jax.named_scope(f"mw{k}{r}"):
-            arrived(mrs.at[k, r], mrecv.at[k, r])
-        both = rsend[k, r, mate_far].astype(F32) + mrecv[k, r].astype(F32)
+            arrived(mrs.at[r], mrecv.at[r])
+        both = rsend[k, r, mate_far].astype(F32) + mrecv[r].astype(F32)
         rsend[k, r, mate_far] = both.astype(BF16)
         dest = (s, mate_far * 2 + c, d)
         rc(rsend.at[k, r, mate_far], rrecv.at[k, r, y], s_r, rrs.at[k, r], dest).start()
 
     def zcopy(r, sec):
-        cs = block(r)
-        return rc(obuf.at[0, :, cs], xin.at[1, :, cs], s_z, zrs.at[r], (sec, i, d))
+        return rc(obuf.at[0, r], xin.at[1, r], s_z, zrs.at[r], (sec, i, d))
 
     def combine(k, r):
-        cs = block(r)
         with jax.named_scope(f"rw{k}{r}"):
             arrived(rrs.at[k, r], rrecv.at[k, r, pl.ds(0, len(near) + urgent(k, r))])
         got = rrecv[k, r].reshape(ny * SLOTS, rwide)
         folded = jnp.concatenate([got[:, q * rstep : (q + 1) * rstep] for q in range(3)], axis=0)
-        res = xin[k, :, cs].astype(F32) + jnp.concatenate(
+        res = xin[k, r].astype(F32) + jnp.concatenate(
             [
                 jnp.dot(mix[k], got, preferred_element_type=F32),
                 jnp.dot(mixs[k], folded, preferred_element_type=F32),
             ],
             axis=1,
         )
-        obuf[k, :, cs] = res.astype(BF16)
-        pltpu.make_async_copy(obuf.at[k, :, cs], out.at[k, :, cs], lsem.at[6 + k]).start()
+        obuf[k, r] = res.astype(BF16)
+        for natural, local in pieces(r):
+            pltpu.make_async_copy(obuf.at[k, r, :, local], out.at[k, :, natural], lsem.at[6 + k]).start()
         if k == 0:
 
             @pl.when(s < nsec - 1)
@@ -425,13 +443,13 @@
 
                 @pl.when(s == 0)
                 def _():
-                    l_fresh.wait()
+                    pltpu.make_async_copy(xin.at[1], xin.at[1], lsem.at[5]).wait()
 
     def cot_arrive(n):
         arrived(crs.at[n - 1], crecv.at[ysrc(n)])
 
     select(0)
-    l_arr.wait()
+    pltpu.make_async_copy(xin.at[0], xin.at[0], lsem.at[0]).wait()
     with jax.named_scope("disp0"):
         dispatch(0)
     select(1)
@@ -481,11 +499,12 @@
     with jax.named_scope("gu0"):
         h = gate_up(0, squares)
     multiply(0, 0, h)
+    pack(0, 0)
+    straight(0, 0)
     with jax.named_scope("fw2"):
         forward_w(2)
+    multiply(0, 1, h)
     share_hidden(0)
-    pack(0, 0)
-    straight(0, 0)
     with jax.named_scope("cotw"):
         for n in near:
             if n in (far - 1, far + 1):
@@ -497,59 +516,59 @@
                 cot_arrive(n)
         cot_arrive(far)
     share_cot()
-    finish_far(0, 0)
+    pack(0, 1)
+    straight(0, 1)
+    combine(0, 0)
     with jax.named_scope("near2"):
         wait_near(2)
-    for r in (1, 2):
-        multiply(0, r, h)
-    for r in (1, 2):
-        pack(0, r)
-    for r in (1, 2):
-        straight(0, r)
-    combine(0, 0)
-    finish_far(0, 1)
-    finish_far(0, 2)
+    multiply(0, 2, h)
+    pack(0, 2)
+    straight(0, 2)
+    combine(0, 1)
+    zwait(0)
+    dispatch(1)
     with jax.named_scope("far2"):
         wait_far(2)
     multiply(0, 3, h)
     pack(0, 3)
     straight(0, 3)
-    combine(0, 1)
     combine(0, 2)
-
-    zwait(0)
-    dispatch(1)
+    zwait(1)
+    dispatch(2)
+
+    with jax.named_scope("rel1"):
+        relay(1)
     combine(0, 3)
     with jax.named_scope("fh0"):
         forward_hidden(0)
-    for r in (1, 2):
-        zwait(r)
-        dispatch(r + 1)
-    with jax.named_scope("rel1"):
-        relay(1)
     with jax.named_scope("fc"):
         forward_cot()
+    zwait(2)
+    dispatch(3)
+    with jax.named_scope("spr1"):
+        spread(1)
+        spread_far(1)
+    with jax.named_scope("rel2"):
+        relay(2)
     zwait(3)
     dispatch(4)
-    with jax.named_scope("rel23"):
-        relay(2)
-        relay(3)
-    with jax.named_scope("spr123"):
-        spread(1)
+    with jax.named_scope("spr2"):
         spread(2)
+    with jax.named_scope("sprf2"):
+        spread_far(2)
+    with jax.named_scope("spr3"):
         spread(3)
-        spread_far(1)
-        spread_far(2)
     squares = []
     for r in range(2):
         wait_spread(r + 1)
         squares.append(unpack(1, r))
         project(r)
+    with jax.named_scope("sprf3"):
+        spread_far(3)
     with jax.named_scope("spr4"):
         spread(4)
+    with jax.named_scope("sprf4"):
         spread_far(4)
-    with jax.named_scope("spr3"):
-        spread_far(3)
     with jax.named_scope("wspr3"):
         wait_spread(3)
     squares.append(unpack(1, 2))
@@ -571,17 +590,17 @@
         pack(1, r)
     for r in range(1, ndp):
         straight(1, r)
+    with jax.named_scope("sc"):
+        spread_cot()
     finish_far(1, 0)
     with jax.named_scope("fh1"):
         forward_hidden(1)
     for r in range(1, ndp):
         finish_far(1, r)
-
-    with jax.named_scope("sc"):
-        spread_cot()
     with jax.named_scope("wsc"):
         arrived(cdr, cotx.at[1])
-    for k in range(2):
+
+    def grad(k):
         with jax.named_scope(f"wh{k}"):
             wait_hidden(k)
         with jax.named_scope(f"grad{k}"):
@@ -594,10 +613,15 @@
                     gacc[...] = add
                 else:
                     gacc[...] += add
+
+    grad(0)
+    combine(1, 0)
+    combine(1, 1)
+    grad(1)
     gout = pltpu.make_async_copy(gacc, grad_out, lsem.at[8])
     gout.start()
-    for r in range(ndp):
-        combine(1, r)
+    combine(1, 2)
+    combine(1, 3)
     with jax.named_scope("tail"):
         drain(s_w, wbuf.at[:, :, pl.ds(0, 3 * cols)])
         drain(s_t, trecv.at[0])
@@ -608,10 +632,9 @@
         drain(s_x, cstage)
         drain(s_h, hid.at[:, pl.ds(0, 3)])
         drain(s_d, drecv)
-        drain(s_m, mrecv.at[0, pl.ds(0, ndp - 1)])
-        drain(s_m, mrecv.at[1])
-        drain(s_r, rrecv.at[:, :, pl.ds(0, len(near))])
-        drain(s_r, rrecv.at[0, 0, 0])
+        drain(s_m, mrecv)
+        drain(s_r, rrecv.at[0, :, pl.ds(0, len(near) + 1)])
+        drain(s_r, rrecv.at[1, :, pl.ds(0, len(near))])
     with jax.named_scope("zs"):
 
         @pl.when(s < nsec - 1)
@@ -621,7 +644,7 @@
     with jax.named_scope("outw"):
         gout.wait()
         for k in range(2):
-            pltpu.make_async_copy(obuf.at[k], out.at[k], lsem.at[6 + k]).wait()
+            pltpu.make_async_copy(obuf.at[k], obuf.at[k], lsem.at[6 + k]).wait()
 
 
 def store_body(out, grad, out_hbm, grad_hbm, sem):
@@ -656,7 +679,7 @@
         in_specs=[hbm_spec] * 9,
         out_specs=(any_spec, any_spec),
         scratch_shapes=[
-            pltpu.VMEM((2, tok, width), BF16),
+            pltpu.VMEM((2, ndp, tok, cols), BF16),
             pltpu.VMEM((2, tok, width), BF16),
             pltpu.VMEM((3, hidn, width), BF16),
             pltpu.VMEM((2, flight, ndp, SLOTS, rwide), BF16),
@@ -672,7 +695,7 @@
             pltpu.VMEM((2, ndp, rows // 2, cols), BF16),
             pltpu.VMEM((ndp, rows // 2, cols), F32),
             pltpu.VMEM((2, ndp, ny, SLOTS, rwide), BF16),
-            pltpu.VMEM((2, ndp, SLOTS, rwide), BF16),
+            pltpu.VMEM((ndp, SLOTS, rwide), BF16),
             pltpu.VMEM((2, ndp, ny, SLOTS, rwide), BF16),
             pltpu.VMEM(routes_t.shape, jnp.int32),
             pltpu.VMEM(gates_t.shape, BF16),
@@ -681,14 +704,14 @@
             pltpu.VMEM((2, 3, flight * SLOTS, 2 * tok), BF16),
             pltpu.VMEM((2, tok, ny * SLOTS), BF16),
             pltpu.VMEM((2, tok, 3 * ny * SLOTS), BF16),
-            pltpu.VMEM((2, tok, width), BF16),
+            pltpu.VMEM((2, ndp, tok, cols), BF16),
             pltpu.VMEM((hidn, cols), F32),
             dma((12,)), dma((9,)),
             dma((3, 2)), dma((3,)), dma((3,)),
             dma((1 + ndp, ny - 1)), dma((1 + ndp,)),
             dma((ny - 1,)), dma((2,)), dma((2,)), dma(()), dma(()),
             dma((2, 2)), dma((2,)), dma((2,)),
-            dma((2, ndp)), dma((2, ndp)), dma((2, ndp)), dma((ndp,)),
+            dma((2, ndp)), dma((ndp,)), dma((2, ndp)), dma((ndp,)),
         ],
         compiler_params=pltpu.CompilerParams(
             collective_id=0, has_side_effects=True, vmem_limit_bytes=24 * 1024 * 1024

time: 79.7 us -> 77.4 us (0.971); the launches traced: 78.5 us -> 77.3 us
  Pallas kernels: 77.9 us -> 76.7 us
    pallas_call x1, Pallas kernels: 76.8 us -> 75.6 us  [local(): pl.pallas_call(functools.partial(kernel_body, nsec, nexp, ndp), name='moe...]
where the time goes in v5:
time: 77.4 us; the launch traced here: 77.3 us
  Pallas kernels  76.7 us (99%)
    pallas_call x1, Pallas kernels, local(): pl.pallas_call(functools.partial(kernel_body, nsec, nexp, ndp), name='moe...  75.6 us

profile of v5, /device:TPU:1, one launch (start us, length us, event | category | flops | bytes accessed | tf_op | source)
XLA Modules:
  0.0 77.3 jit_solution(6055207760870965919)
XLA Ops:
  0.6 75.6 %moe_relay.1 = (bf16[2,64,2048]{2,1,0:T(8,128)(2,1)S(1)}, f32[352,512]{1,0:T(8,128)S(1)}) custom-call(bf16[64,2048]{1,0:T(8,128)(2,1)} %bitcast.18, bf16[64,2048]{1,0:T(8,128)(2,1)} %bitcast.19, s32[6,2,64]{2,1,0:T(2,128)} %bitcast.20, bf16[6,2,64]{2,1,0:T(2,128)(2,1)} %bitcast.21, bf16[2,64,2048]{2,1,0:T(8,128)(2,1)} %bitcast.14, f32[1,2048]{1,0:T(1,128)} %gain.1, ...), custom_call_target="tpu_custom_call" | custom-call | tf_op jit(solution)/shard_map/moe_relay/pallas_call | solution.py:672
  76.3 1.1 %store.1 = (bf16[2,64,2048]{2,1,0:T(8,128)(2,1)}, f32[352,512]{1,0:T(8,128)}) custom-call(bf16[2,64,2048]{2,1,0:T(8,128)(2,1)S(1)} %get-tuple-element.6.out, f32[352,512]{1,0:T(8,128)S(1)} %get-tuple-element.7.grad), custom_call_target="tpu_custom_call" | custom-call | tf_op jit(solution)/shard_map/store/pallas_call | solution.py:727

commit v6 on v5

--- a/solution.py
+++ b/solution.py
@@ -10,7 +10,7 @@
 SPLIT = 4
 CAP = 12
 SLOTS = 16
-DIRECT = 3
+DIRECT = 2
 NEAR = (3, 5, 2, 6, 1, 7)
 MESH = pl.DeviceIdType.MESH
 NT = (((1,), (1,)), ((), ()))
@@ -548,8 +548,6 @@
     with jax.named_scope("spr1"):
         spread(1)
         spread_far(1)
-    with jax.named_scope("rel2"):
-        relay(2)
     zwait(3)
     dispatch(4)
     with jax.named_scope("spr2"):
@@ -588,15 +586,17 @@
     multiply(1, 3, h)
     for r in range(1, ndp):
         pack(1, r)
-    for r in range(1, ndp):
-        straight(1, r)
+    straight(1, 1)
+    finish_far(1, 0)
     with jax.named_scope("sc"):
         spread_cot()
-    finish_far(1, 0)
     with jax.named_scope("fh1"):
         forward_hidden(1)
-    for r in range(1, ndp):
-        finish_far(1, r)
+    finish_far(1, 1)
+    finish_far(1, 2)
+    straight(1, 2)
+    finish_far(1, 3)
+    straight(1, 3)
     with jax.named_scope("wsc"):
         arrived(cdr, cotx.at[1])
 

time: 77.4 us -> 76.2 us (0.984); the launches traced: 77.3 us -> 75.3 us
  Pallas kernels: 76.7 us -> 74.6 us
    pallas_call x1, Pallas kernels: 75.6 us -> 73.6 us  [local(): pl.pallas_call(functools.partial(kernel_body, nsec, nexp, ndp), name='moe...]
where the time goes in v6:
time: 76.2 us; the launch traced here: 75.3 us
  Pallas kernels  74.6 us (98%)
    pallas_call x1, Pallas kernels, local(): pl.pallas_call(functools.partial(kernel_body, nsec, nexp, ndp), name='moe...  73.6 us

profile of v6, /device:TPU:1, one launch (start us, length us, event | category | flops | bytes accessed | tf_op | source)
XLA Modules:
  0.0 75.3 jit_solution(18303133649242879007)
XLA Ops:
  0.6 73.6 %moe_relay.1 = (bf16[2,64,2048]{2,1,0:T(8,128)(2,1)S(1)}, f32[352,512]{1,0:T(8,128)S(1)}) custom-call(bf16[64,2048]{1,0:T(8,128)(2,1)} %bitcast.18, bf16[64,2048]{1,0:T(8,128)(2,1)} %bitcast.19, s32[6,2,64]{2,1,0:T(2,128)} %bitcast.20, bf16[6,2,64]{2,1,0:T(2,128)(2,1)} %bitcast.21, bf16[2,64,2048]{2,1,0:T(8,128)(2,1)} %bitcast.14, f32[1,2048]{1,0:T(1,128)} %gain.1, ...), custom_call_target="tpu_custom_call" | custom-call | tf_op jit(solution)/shard_map/moe_relay/pallas_call | solution.py:672
  74.2 1.1 %store.1 = (bf16[2,64,2048]{2,1,0:T(8,128)(2,1)}, f32[352,512]{1,0:T(8,128)}) custom-call(bf16[2,64,2048]{2,1,0:T(8,128)(2,1)S(1)} %get-tuple-element.6.out, f32[352,512]{1,0:T(8,128)S(1)} %get-tuple-element.7.grad), custom_call_target="tpu_custom_call" | custom-call | tf_op jit(solution)/shard_map/store/pallas_call | solution.py:727

commit v7 on v6

--- a/solution.py
+++ b/solution.py
@@ -620,8 +620,6 @@
     grad(1)
     gout = pltpu.make_async_copy(gacc, grad_out, lsem.at[8])
     gout.start()
-    combine(1, 2)
-    combine(1, 3)
     with jax.named_scope("tail"):
         drain(s_w, wbuf.at[:, :, pl.ds(0, 3 * cols)])
         drain(s_t, trecv.at[0])
@@ -633,18 +631,20 @@
         drain(s_h, hid.at[:, pl.ds(0, 3)])
         drain(s_d, drecv)
         drain(s_m, mrecv)
-        drain(s_r, rrecv.at[0, :, pl.ds(0, len(near) + 1)])
-        drain(s_r, rrecv.at[1, :, pl.ds(0, len(near))])
     with jax.named_scope("zs"):
 
         @pl.when(s < nsec - 1)
         def _():
             drain(s_z, obuf.at[0])
+    pltpu.make_async_copy(obuf.at[0], obuf.at[0], lsem.at[6]).wait()
+    combine(1, 2)
+    combine(1, 3)
+    drain(s_r, rrecv.at[0, :, pl.ds(0, len(near) + 1)])
+    drain(s_r, rrecv.at[1, :, pl.ds(0, len(near))])
 
     with jax.named_scope("outw"):
         gout.wait()
-        for k in range(2):
-            pltpu.make_async_copy(obuf.at[k], obuf.at[k], lsem.at[6 + k]).wait()
+        pltpu.make_async_copy(obuf.at[1], obuf.at[1], lsem.at[7]).wait()
 
 
 def store_body(out, grad, out_hbm, grad_hbm, sem):

time: 76.2 us -> 76.2 us (level)
  no operation moved by 1% of the time
where the time goes in v7:
time: 76.2 us; the launch traced here: 75.2 us
  Pallas kernels  74.6 us (98%)
    pallas_call x1, Pallas kernels, local(): pl.pallas_call(functools.partial(kernel_body, nsec, nexp, ndp), name='moe...  73.6 us

profile of v7, /device:TPU:1, one launch (start us, length us, event | category | flops | bytes accessed | tf_op | source)
XLA Modules:
  0.0 75.2 jit_solution(1815904418516654522)
XLA Ops:
  0.6 73.6 %moe_relay.1 = (bf16[2,64,2048]{2,1,0:T(8,128)(2,1)S(1)}, f32[352,512]{1,0:T(8,128)S(1)}) custom-call(bf16[64,2048]{1,0:T(8,128)(2,1)} %bitcast.18, bf16[64,2048]{1,0:T(8,128)(2,1)} %bitcast.19, s32[6,2,64]{2,1,0:T(2,128)} %bitcast.20, bf16[6,2,64]{2,1,0:T(2,128)(2,1)} %bitcast.21, bf16[2,64,2048]{2,1,0:T(8,128)(2,1)} %bitcast.14, f32[1,2048]{1,0:T(1,128)} %gain.1, ...), custom_call_target="tpu_custom_call" | custom-call | tf_op jit(solution)/shard_map/moe_relay/pallas_call | solution.py:672
  74.2 1.1 %store.1 = (bf16[2,64,2048]{2,1,0:T(8,128)(2,1)}, f32[352,512]{1,0:T(8,128)}) custom-call(bf16[2,64,2048]{2,1,0:T(8,128)(2,1)S(1)} %get-tuple-element.6.out, f32[352,512]{1,0:T(8,128)S(1)} %get-tuple-element.7.grad), custom_call_target="tpu_custom_call" | custom-call | tf_op jit(solution)/shard_map/store/pallas_call | solution.py:727
